TPU v7x, 512 devices: a whole 4x4x16 slice. The times are simulated.
512 devices in a mesh: tm: 4 (over y), row: 16 (over z), col: 8 (over x, core).
Axes of the slice: x: 4, y: 4, z: 16, core: 2. Of those that a mesh axis runs over, the one named last changes fastest.
Arguments:
- noisy_video: float32 [16, 2048, 2048], P('tm', 'row', 'col'), may hold values from -6 to 6
- fidelity: float32 [16, 2048, 2048], P('tm', 'row', 'col'), may hold values from 0.5 to 12, as said below
Outputs:
- denoised: float32 [16, 2048, 2048], P('tm', 'row', 'col')
- gaps: float32 [3], replicated
Inputs may be any that keep to these rules, and one draw needn't show every extreme that they name: `fidelity`: positive, larger on average toward later rows.
All inputs are finite; a program needn't handle non-finite values.
Results may differ from a plain program's by a relative error of at most 0.0001.
Values sent between devices are 32-bit elements; how exact they have to be, the bound alone decides.
A program may use at most 64 MiB of HBM per device.

v0:
```python
import jax
import jax.numpy as jnp
from jax import lax
from jax.sharding import Mesh
from jax.sharding import PartitionSpec as P

ITERS = 3
COL = ("col_0", "col_1")
TM_ROW_COL = ("tm", "row", "col_0", "col_1")


sigma_step = 0.28
tau_step = 0.28


def shifted(block, axis, distance):
    devices = range(lax.axis_size(axis))
    route = [(i - distance, i) for i in devices if i - distance in devices]
    return lax.ppermute(block, axis, route)


def one_axis_at_a_time(value, axes):
    for axis in axes:
        value = lax.psum(value, axis)
    return value


def ahead_diff(field, ghost, axis, is_last):
    count = field.shape[axis]
    inner = lax.slice_in_dim(field, 1, count, axis=axis)
    own_last = lax.slice_in_dim(field, count - 1, count, axis=axis)
    following = jnp.concatenate([inner, jnp.where(is_last, own_last, ghost)], axis=axis)
    return following - field


def behind_diff(comp, ghost, axis):
    count = comp.shape[axis]
    before = jnp.concatenate([ghost, lax.slice_in_dim(comp, 0, count - 1, axis=axis)], axis=axis)
    return comp - before


def project(duals, grads):
    moved_time = duals[0] + sigma_step * grads[0]
    moved_rows = duals[1] + sigma_step * grads[1]
    moved_cols = duals[2] + sigma_step * grads[2]
    length = jnp.sqrt(moved_time * moved_time + moved_rows * moved_rows + moved_cols * moved_cols)
    scale = jnp.maximum(1.0, length)
    return [moved_time / scale, moved_rows / scale, moved_cols / scale]


def on_device(noisy_video, fidelity):
    frames, rows_dev, cols_dev = noisy_video.shape
    cells = float(
        noisy_video.size * lax.axis_size("tm") * lax.axis_size("row") * lax.axis_size(COL)
    )
    last_frame = lax.axis_index("tm") == lax.axis_size("tm") - 1
    last_row = lax.axis_index("row") == lax.axis_size("row") - 1
    last_col = lax.axis_index(COL) == lax.axis_size(COL) - 1
    field = noisy_video
    ubar_field = noisy_video
    zero_dual = jnp.zeros_like(noisy_video)
    duals = [zero_dual, zero_dual, zero_dual]
    grad_u = None
    local_gaps = []
    for iteration in range(ITERS):
        ghost_time = shifted(ubar_field[0:1], "tm", -1)
        ghost_rows = shifted(ubar_field[:, 0:1], "row", -1)
        ghost_cols = shifted(ubar_field[:, :, 0:1], COL, -1)
        grads = [
            ahead_diff(ubar_field, ghost_time, 0, last_frame),
            ahead_diff(ubar_field, ghost_rows, 1, last_row),
            ahead_diff(ubar_field, ghost_cols, 2, last_col),
        ]
        duals = project(duals, grads)
        prev_time = shifted(duals[0][frames - 1 :], "tm", 1)
        prev_rows = shifted(duals[1][:, rows_dev - 1 :], "row", 1)
        prev_cols = shifted(duals[2][:, :, cols_dev - 1 :], COL, 1)
        diverge = (
            behind_diff(duals[0], prev_time, 0)
            + behind_diff(duals[1], prev_rows, 1)
            + behind_diff(duals[2], prev_cols, 2)
        )
        if iteration == 0:
            grad_u = grads
        else:
            grad_u = [
                0.5 * (grads[0] + grad_u[0]),
                0.5 * (grads[1] + grad_u[1]),
                0.5 * (grads[2] + grad_u[2]),
            ]
        total_var = jnp.sqrt(grad_u[0] * grad_u[0] + grad_u[1] * grad_u[1] + grad_u[2] * grad_u[2])
        resid = field - noisy_video
        term = (
            0.5 * fidelity * resid * resid
            + total_var
            + diverge * diverge / (2.0 * fidelity)
            + noisy_video * diverge
        )
        local_sum = jnp.sum(term)
        local_gaps.append(local_sum)
        new_field = (field + tau_step * diverge + tau_step * fidelity * noisy_video) / (
            1.0 + tau_step * fidelity
        )
        ubar_field = 2.0 * new_field - field
        field = new_field
    gaps = one_axis_at_a_time(jnp.stack(local_gaps), TM_ROW_COL) / cells
    return (field, gaps)


def solution(mesh):
    finer = Mesh(
        mesh.devices.reshape(mesh.shape["tm"], mesh.shape["row"], 4, 2),
        ("tm", "row", "col_0", "col_1"),
    )
    placed = (P("tm", "row", COL), P("tm", "row", COL))
    return jax.shard_map(
        on_device,
        mesh=finer,
        in_specs=placed,
        out_specs=(P("tm", "row", COL), P()),
        check_vma=False,
    )
```

profile of v0, /device:TPU:1, one launch (start us, length us, event | category | flops | bytes accessed | tf_op | source)
XLA Modules:
  0.0 153.8 jit_solution(11274911746246239184)
XLA Ops:
  0.6 0.0 copy-start
  0.6 1.0 slice.143
  1.7 8.7 %collective-permute-start.2 = (f32[4,128,1]{2,1,0:T(8,128)S(1)}, f32[4,128,1]{2,1,0:T(8,128)S(1)}, u32[]{:S(2)}, u32[]{:S(2)}) collective-permute-start(f32[4,128,1]{2,1,0:T(8,128)S(1)} %slice.143), channel_id=1, source_target_pairs={{1,0},{2,1},{3,2},{4,3},{5,4},{6,5},{7,6},{9,8},{10,9},{11,10},{12... | collective-permute-start | bytes 6152 | tf_op jit(solution)/shard_map/ppermute | solution.py:19
  10.5 1.3 collective-permute-start.1
  11.8 1.3 collective-permute-start
  13.1 0.2 slice.141
  13.4 0.0 collective-permute-done.2
  13.4 0.1 slice_select_fusion.2
  13.5 1.4 collective-permute-done.1
  15.0 3.9 %collective-permute-done = f32[1,128,256]{2,1,0:T(8,128)S(1)} collective-permute-done((f32[1,128,256]{2,1,0:T(8,128)S(1)}, f32[1,128,256]{2,1,0:T(8,128)S(1)}, u32[]{:S(2)}, u32[]{:S(2)}) %collective-permute-start) | collective-permute-done | bytes 131104 | tf_op jit(solution)/shard_map/ppermute | solution.py:19
  18.9 0.5 multiply_divide_fusion.2
  19.4 1.4 collective-permute-start.3
  20.8 4.1 %collective-permute-start.4 = (f32[4,1,256]{2,1,0:T(1,128)S(1)}, f32[4,1,256]{2,1,0:T(1,128)S(1)}, u32[]{:S(2)}, u32[]{:S(2)}) collective-permute-start(f32[4,1,256]{2,1,0:T(1,128)S(1)} %slice.182), channel_id=1, source_target_pairs={{0,8},{8,16},{16,24},{24,32},{32,40},{40,48},{48,56},{56,64},{64,7... | collective-permute-start | bytes 12296 | tf_op jit(solution)/shard_map/ppermute | solution.py:19
  24.9 0.1 slice.184
  25.0 0.0 copy-start.1
  25.0 2.1 %collective-permute-start.5 = (f32[4,128,1]{2,1,0:T(8,128)S(1)}, f32[4,128,1]{2,1,0:T(8,128)S(1)}, u32[]{:S(2)}, u32[]{:S(2)}) collective-permute-start(f32[4,128,1]{2,1,0:T(8,128)S(1)} %slice.184), channel_id=1, source_target_pairs={{0,1},{1,2},{2,3},{3,4},{4,5},{5,6},{6,7},{8,9},{9,10},{10,11},{11... | collective-permute-start | bytes 6152 | tf_op jit(solution)/shard_map/ppermute | solution.py:19
  27.1 3.3 %collective-permute-done.5 = f32[4,128,1]{2,1,0:T(8,128)S(1)} collective-permute-done((f32[4,128,1]{2,1,0:T(8,128)S(1)}, f32[4,128,1]{2,1,0:T(8,128)S(1)}, u32[]{:S(2)}, u32[]{:S(2)}) %collective-permute-start.5) | collective-permute-done | bytes 2080 | tf_op jit(solution)/shard_map/ppermute | solution.py:19
  30.4 0.0 collective-permute-done.4
  30.4 0.0 collective-permute-done.3
  30.4 0.5 multiply_subtract_fusion.1
  30.9 1.9 %collective-permute-start.8 = (f32[4,128,1]{2,1,0:T(8,128)S(1)}, f32[4,128,1]{2,1,0:T(8,128)S(1)}, u32[]{:S(2)}, u32[]{:S(2)}) collective-permute-start(f32[4,128,1]{2,1,0:T(8,128)S(1)} %slice.194), channel_id=1, source_target_pairs={{1,0},{2,1},{3,2},{4,3},{5,4},{6,5},{7,6},{9,8},{10,9},{11,10},{12... | collective-permute-start | bytes 6152 | tf_op jit(solution)/shard_map/ppermute | solution.py:19
  32.9 0.2 slice.192
  33.1 1.3 collective-permute-start.7
  34.4 1.3 collective-permute-start.6
  35.7 3.6 %collective-permute-done.8 = f32[4,128,1]{2,1,0:T(8,128)S(1)} collective-permute-done((f32[4,128,1]{2,1,0:T(8,128)S(1)}, f32[4,128,1]{2,1,0:T(8,128)S(1)}, u32[]{:S(2)}, u32[]{:S(2)}) %collective-permute-start.8) | collective-permute-done | bytes 2080 | tf_op jit(solution)/shard_map/ppermute | solution.py:19
  39.3 0.1 slice_select_fusion.1
  39.5 0.0 collective-permute-done.7
  39.5 0.7 collective-permute-done.6
  40.2 0.5 fusion.20
  40.7 0.2 fusion.18
  40.9 2.1 %collective-permute-start.9 = (f32[1,128,256]{2,1,0:T(8,128)S(1)}, f32[1,128,256]{2,1,0:T(8,128)S(1)}, u32[]{:S(2)}, u32[]{:S(2)}) collective-permute-start(f32[1,128,256]{2,1,0:T(8,128)S(1)} %slice.195), channel_id=1, source_target_pairs={{0,128},{128,256},{256,384},{1,129},{129,257},{257,385},{2,130},{1... | collective-permute-start | bytes 393224 | tf_op jit(solution)/shard_map/ppermute | solution.py:19
  43.0 4.2 %collective-permute-start.10 = (f32[4,1,256]{2,1,0:T(1,128)S(1)}, f32[4,1,256]{2,1,0:T(1,128)S(1)}, u32[]{:S(2)}, u32[]{:S(2)}) collective-permute-start(f32[4,1,256]{2,1,0:T(1,128)S(1)} %slice.197), channel_id=1, source_target_pairs={{0,8},{8,16},{16,24},{24,32},{32,40},{40,48},{48,56},{56,64},{64,7... | collective-permute-start | bytes 12296 | tf_op jit(solution)/shard_map/ppermute | solution.py:19
  47.2 0.1 slice.199
  47.3 7.0 %collective-permute-start.11 = (f32[4,128,1]{2,1,0:T(8,128)S(1)}, f32[4,128,1]{2,1,0:T(8,128)S(1)}, u32[]{:S(2)}, u32[]{:S(2)}) collective-permute-start(f32[4,128,1]{2,1,0:T(8,128)S(1)} %slice.199), channel_id=1, source_target_pairs={{0,1},{1,2},{2,3},{3,4},{4,5},{5,6},{6,7},{8,9},{9,10},{10,11},{11... | collective-permute-start | bytes 6152 | tf_op jit(solution)/shard_map/ppermute | solution.py:19
  54.4 3.3 %collective-permute-done.11 = f32[4,128,1]{2,1,0:T(8,128)S(1)} collective-permute-done((f32[4,128,1]{2,1,0:T(8,128)S(1)}, f32[4,128,1]{2,1,0:T(8,128)S(1)}, u32[]{:S(2)}, u32[]{:S(2)}) %collective-permute-start.11) | collective-permute-done | bytes 2080 | tf_op jit(solution)/shard_map/ppermute | solution.py:19
  57.7 0.0 collective-permute-done.10
  57.7 0.0 collective-permute-done.9
  57.7 1.9 %fusion.3 = (f32[]{:T(128)}, f32[]{:T(128)}, f32[4,128,256]{2,1,0:T(8,128)S(1)}) fusion(f32[4,128,256]{2,1,0:T(8,128)S(1)} %copy-done, f32[4,128,256]{2,1,0:T(8,128)S(1)} %get-tuple-element.17, f32[4,128,256]{2,1,0:T(8,128)S(1)} %copy-done.1, f32[1,128,256]{2,1,0:T(8,128)S(1)} %slice_select_fusion.5, f32[3,128,256]{2,1,0:T(8,128)S(1)} %slice.135, ...), kind=kLoop, calls=%fused_computation.6 | loop fusion | flops 7733246 | bytes 8388616 | tf_op jit(solution)/shard_map/reduce_sum | solution.py:99
  59.6 0.3 multiply_subtract_fusion
  59.9 1.9 %collective-permute-start.14 = (f32[4,128,1]{2,1,0:T(8,128)S(1)}, f32[4,128,1]{2,1,0:T(8,128)S(1)}, u32[]{:S(2)}, u32[]{:S(2)}) collective-permute-start(f32[4,128,1]{2,1,0:T(8,128)S(1)} %slice.209), channel_id=1, source_target_pairs={{1,0},{2,1},{3,2},{4,3},{5,4},{6,5},{7,6},{9,8},{10,9},{11,10},{12... | collective-permute-start | bytes 6152 | tf_op jit(solution)/shard_map/ppermute | solution.py:19
  61.9 0.2 slice.207
  62.1 1.3 collective-permute-start.13
  63.4 1.3 collective-permute-start.12
  64.7 3.6 %collective-permute-done.14 = f32[4,128,1]{2,1,0:T(8,128)S(1)} collective-permute-done((f32[4,128,1]{2,1,0:T(8,128)S(1)}, f32[4,128,1]{2,1,0:T(8,128)S(1)}, u32[]{:S(2)}, u32[]{:S(2)}) %collective-permute-start.14) | collective-permute-done | bytes 2080 | tf_op jit(solution)/shard_map/ppermute | solution.py:19
  68.3 0.1 slice_select_fusion
  68.5 0.0 collective-permute-done.13
  68.5 0.7 collective-permute-done.12
  69.2 0.5 fusion.23
  69.7 0.3 fusion.21
  70.0 1.6 %collective-permute-start.15 = (f32[1,128,256]{2,1,0:T(8,128)S(1)}, f32[1,128,256]{2,1,0:T(8,128)S(1)}, u32[]{:S(2)}, u32[]{:S(2)}) collective-permute-start(f32[1,128,256]{2,1,0:T(8,128)S(1)} %slice.210), channel_id=1, source_target_pairs={{0,128},{128,256},{256,384},{1,129},{129,257},{257,385},{2,130},{1... | collective-permute-start | bytes 393224 | tf_op jit(solution)/shard_map/ppermute | solution.py:19
  71.7 4.5 %collective-permute-start.16 = (f32[4,1,256]{2,1,0:T(1,128)S(1)}, f32[4,1,256]{2,1,0:T(1,128)S(1)}, u32[]{:S(2)}, u32[]{:S(2)}) collective-permute-start(f32[4,1,256]{2,1,0:T(1,128)S(1)} %slice.212), channel_id=1, source_target_pairs={{0,8},{8,16},{16,24},{24,32},{32,40},{40,48},{48,56},{56,64},{64,7... | collective-permute-start | bytes 12296 | tf_op jit(solution)/shard_map/ppermute | solution.py:19
  76.2 0.1 slice.214
  76.3 6.7 %collective-permute-start.17 = (f32[4,128,1]{2,1,0:T(8,128)S(1)}, f32[4,128,1]{2,1,0:T(8,128)S(1)}, u32[]{:S(2)}, u32[]{:S(2)}) collective-permute-start(f32[4,128,1]{2,1,0:T(8,128)S(1)} %slice.214), channel_id=1, source_target_pairs={{0,1},{1,2},{2,3},{3,4},{4,5},{5,6},{6,7},{8,9},{9,10},{10,11},{11... | collective-permute-start | bytes 6152 | tf_op jit(solution)/shard_map/ppermute | solution.py:19
  83.1 3.3 %collective-permute-done.17 = f32[4,128,1]{2,1,0:T(8,128)S(1)} collective-permute-done((f32[4,128,1]{2,1,0:T(8,128)S(1)}, f32[4,128,1]{2,1,0:T(8,128)S(1)}, u32[]{:S(2)}, u32[]{:S(2)}) %collective-permute-start.17) | collective-permute-done | bytes 2080 | tf_op jit(solution)/shard_map/ppermute | solution.py:19
  86.3 0.0 collective-permute-done.16
  86.3 0.0 collective-permute-done.15
  86.3 2.8 %fusion.11 = (f32[]{:T(128)}, f32[4,128,256]{2,1,0:T(8,128)}) fusion(f32[4,128,256]{2,1,0:T(8,128)S(1)} %copy-done, f32[4,128,256]{2,1,0:T(8,128)S(1)} %get-tuple-element.9, f32[4,128,256]{2,1,0:T(8,128)S(1)} %get-tuple-element.10, f32[4,128,256]{2,1,0:T(8,128)S(1)} %copy-done.1, f32[4,128,256]{2,1,0:T(8,128)S(1)} %get-tuple-element.15, ...), kind=kLoop, calls=%fused_computation.14 | loop fusion | flops 7340031 | bytes 11010052 | tf_op jit(solution)/shard_map/reduce_sum | solution.py:99
  89.1 2.0 %pad_maximum_fusion = f32[3]{0:T(128)S(1)} fusion(f32[1]{0:T(128)} %bitcast.2, f32[1]{0:T(128)} %bitcast.1, f32[1]{0:T(128)} %bitcast), kind=kLoop, calls=%fused_computation.76 | loop fusion | flops 6 | bytes 24 | tf_op jit(solution)/shard_map/stack | solution.py:106
  91.1 6.0 %psum.28 = f32[3]{0:T(128)S(1)} all-reduce(f32[3]{0:T(128)S(1)} %pad_maximum_fusion), channel_id=1, replica_groups=mesh['tm'=4,'row'=16,'col_0'=4,'col_1'=2] {'tm'}, use_global_device_ids=true, to_apply=%region_3.4 | all-reduce | flops 3 | bytes 24 | tf_op jit(solution)/shard_map/psum | solution.py:24
  97.1 31.1 %psum.29 = f32[3]{0:T(128)S(1)} all-reduce(f32[3]{0:T(128)S(1)} %psum.28), channel_id=1, replica_groups=mesh['tm'=4,'row'=16,'col_0'=4,'col_1'=2] {'row'}, use_global_device_ids=true, to_apply=%region_4.5 | all-reduce | flops 3 | bytes 24 | tf_op jit(solution)/shard_map/psum | solution.py:24
  128.2 7.5 %psum.30 = f32[3]{0:T(128)S(1)} all-reduce(f32[3]{0:T(128)S(1)} %psum.29), channel_id=1, replica_groups=mesh['tm'=4,'row'=16,'col_0'=4,'col_1'=2] {'col_0'}, use_global_device_ids=true, to_apply=%region_5.6 | all-reduce | flops 3 | bytes 24 | tf_op jit(solution)/shard_map/psum | solution.py:24
  135.6 2.1 %add_divide_fusion = f32[4,128,256]{2,1,0:T(8,128)} fusion(f32[4,128,256]{2,1,0:T(8,128)} %get-tuple-element.6, f32[4,128,256]{2,1,0:T(8,128)S(1)} %copy-done.1, f32[4,128,256]{2,1,0:T(8,128)S(1)} %copy-done, f32[4,128,256]{2,1,0:T(8,128)S(1)} %get-tuple-element.4, f32[4,128,256]{2,1,0:T(8,128)S(1)} %get-tuple-element.17), kind=kLoop, calls=%fused_computation.42 | loop fusion | flops 1966080 | bytes 3145728 | tf_op jit(solution)/shard_map/div | solution.py:101
  137.8 15.5 %psum.31 = f32[3]{0:T(128)S(1)} all-reduce(f32[3]{0:T(128)S(1)} %psum.30), channel_id=1, replica_groups=mesh['tm'=4,'row'=16,'col_0'=4,'col_1'=2] {'col_1'}, use_global_device_ids=true, to_apply=%region_6.7 | all-reduce | flops 3 | bytes 24 | tf_op jit(solution)/shard_map/psum | solution.py:24
  153.2 0.5 broadcast_multiply_fusion
  (31 shorter events, 0.5 us)
Async XLA Ops:
  0.6 9.8 %copy-start = (f32[4,128,256]{2,1,0:T(8,128)S(1)}, f32[4,128,256]{2,1,0:T(8,128)}, u32[]{:S(2)}) copy-start(f32[4,128,256]{2,1,0:T(8,128)} %param.2) | copy-start | bytes 1572868
  1.7 11.7 %collective-permute-start.2 = (f32[4,128,1]{2,1,0:T(8,128)S(1)}, f32[4,128,1]{2,1,0:T(8,128)S(1)}, u32[]{:S(2)}, u32[]{:S(2)}) collective-permute-start(f32[4,128,1]{2,1,0:T(8,128)S(1)} %slice.143), channel_id=1, source_target_pairs={{1,0},{2,1},{3,2},{4,3},{5,4},{6,5},{7,6},{9,8},{10,9},{11,10},{12... | collective-permute-start | bytes 6152 | tf_op jit(solution)/shard_map/ppermute | solution.py:19
  10.5 4.5 %collective-permute-start.1 = (f32[4,1,256]{2,1,0:T(1,128)S(1)}, f32[4,1,256]{2,1,0:T(1,128)S(1)}, u32[]{:S(2)}, u32[]{:S(2)}) collective-permute-start(f32[4,1,256]{2,1,0:T(1,128)S(1)} %slice.140), channel_id=1, source_target_pairs={{8,0},{16,8},{24,16},{32,24},{40,32},{48,40},{56,48},{64,56},{72,6... | collective-permute-start | bytes 12296 | tf_op jit(solution)/shard_map/ppermute | solution.py:19
  11.8 7.1 %collective-permute-start = (f32[1,128,256]{2,1,0:T(8,128)S(1)}, f32[1,128,256]{2,1,0:T(8,128)S(1)}, u32[]{:S(2)}, u32[]{:S(2)}) collective-permute-start(f32[1,128,256]{2,1,0:T(8,128)S(1)} %slice.137), channel_id=1, source_target_pairs={{128,0},{256,128},{384,256},{129,1},{257,129},{385,257},{130,2},{2... | collective-permute-start | bytes 393224 | tf_op jit(solution)/shard_map/ppermute | solution.py:19
  19.4 11.0 %collective-permute-start.3 = (f32[1,128,256]{2,1,0:T(8,128)S(1)}, f32[1,128,256]{2,1,0:T(8,128)S(1)}, u32[]{:S(2)}, u32[]{:S(2)}) collective-permute-start(f32[1,128,256]{2,1,0:T(8,128)S(1)} %slice.180), channel_id=1, source_target_pairs={{0,128},{128,256},{256,384},{1,129},{129,257},{257,385},{2,130},{1... | collective-permute-start | bytes 393224 | tf_op jit(solution)/shard_map/ppermute | solution.py:19
  20.8 9.6 %collective-permute-start.4 = (f32[4,1,256]{2,1,0:T(1,128)S(1)}, f32[4,1,256]{2,1,0:T(1,128)S(1)}, u32[]{:S(2)}, u32[]{:S(2)}) collective-permute-start(f32[4,1,256]{2,1,0:T(1,128)S(1)} %slice.182), channel_id=1, source_target_pairs={{0,8},{8,16},{16,24},{24,32},{32,40},{40,48},{48,56},{56,64},{64,7... | collective-permute-start | bytes 12296 | tf_op jit(solution)/shard_map/ppermute | solution.py:19
  25.0 5.4 %copy-start.1 = (f32[4,128,256]{2,1,0:T(8,128)S(1)}, f32[4,128,256]{2,1,0:T(8,128)}, u32[]{:S(2)}) copy-start(f32[4,128,256]{2,1,0:T(8,128)} %param.3) | copy-start | bytes 1572868
  25.0 5.4 %collective-permute-start.5 = (f32[4,128,1]{2,1,0:T(8,128)S(1)}, f32[4,128,1]{2,1,0:T(8,128)S(1)}, u32[]{:S(2)}, u32[]{:S(2)}) collective-permute-start(f32[4,128,1]{2,1,0:T(8,128)S(1)} %slice.184), channel_id=1, source_target_pairs={{0,1},{1,2},{2,3},{3,4},{4,5},{5,6},{6,7},{8,9},{9,10},{10,11},{11... | collective-permute-start | bytes 6152 | tf_op jit(solution)/shard_map/ppermute | solution.py:19
  30.9 8.4 %collective-permute-start.8 = (f32[4,128,1]{2,1,0:T(8,128)S(1)}, f32[4,128,1]{2,1,0:T(8,128)S(1)}, u32[]{:S(2)}, u32[]{:S(2)}) collective-permute-start(f32[4,128,1]{2,1,0:T(8,128)S(1)} %slice.194), channel_id=1, source_target_pairs={{1,0},{2,1},{3,2},{4,3},{5,4},{6,5},{7,6},{9,8},{10,9},{11,10},{12... | collective-permute-start | bytes 6152 | tf_op jit(solution)/shard_map/ppermute | solution.py:19
  33.1 6.3 %collective-permute-start.7 = (f32[4,1,256]{2,1,0:T(1,128)S(1)}, f32[4,1,256]{2,1,0:T(1,128)S(1)}, u32[]{:S(2)}, u32[]{:S(2)}) collective-permute-start(f32[4,1,256]{2,1,0:T(1,128)S(1)} %slice.191), channel_id=1, source_target_pairs={{8,0},{16,8},{24,16},{32,24},{40,32},{48,40},{56,48},{64,56},{72,6... | collective-permute-start | bytes 12296 | tf_op jit(solution)/shard_map/ppermute | solution.py:19
  34.4 5.7 %collective-permute-start.6 = (f32[1,128,256]{2,1,0:T(8,128)S(1)}, f32[1,128,256]{2,1,0:T(8,128)S(1)}, u32[]{:S(2)}, u32[]{:S(2)}) collective-permute-start(f32[1,128,256]{2,1,0:T(8,128)S(1)} %slice.188), channel_id=1, source_target_pairs={{128,0},{256,128},{384,256},{129,1},{257,129},{385,257},{130,2},{2... | collective-permute-start | bytes 393224 | tf_op jit(solution)/shard_map/ppermute | solution.py:19
  40.9 16.8 %collective-permute-start.9 = (f32[1,128,256]{2,1,0:T(8,128)S(1)}, f32[1,128,256]{2,1,0:T(8,128)S(1)}, u32[]{:S(2)}, u32[]{:S(2)}) collective-permute-start(f32[1,128,256]{2,1,0:T(8,128)S(1)} %slice.195), channel_id=1, source_target_pairs={{0,128},{128,256},{256,384},{1,129},{129,257},{257,385},{2,130},{1... | collective-permute-start | bytes 393224 | tf_op jit(solution)/shard_map/ppermute | solution.py:19
  43.0 14.7 %collective-permute-start.10 = (f32[4,1,256]{2,1,0:T(1,128)S(1)}, f32[4,1,256]{2,1,0:T(1,128)S(1)}, u32[]{:S(2)}, u32[]{:S(2)}) collective-permute-start(f32[4,1,256]{2,1,0:T(1,128)S(1)} %slice.197), channel_id=1, source_target_pairs={{0,8},{8,16},{16,24},{24,32},{32,40},{40,48},{48,56},{56,64},{64,7... | collective-permute-start | bytes 12296 | tf_op jit(solution)/shard_map/ppermute | solution.py:19
  47.3 10.3 %collective-permute-start.11 = (f32[4,128,1]{2,1,0:T(8,128)S(1)}, f32[4,128,1]{2,1,0:T(8,128)S(1)}, u32[]{:S(2)}, u32[]{:S(2)}) collective-permute-start(f32[4,128,1]{2,1,0:T(8,128)S(1)} %slice.199), channel_id=1, source_target_pairs={{0,1},{1,2},{2,3},{3,4},{4,5},{5,6},{6,7},{8,9},{9,10},{10,11},{11... | collective-permute-start | bytes 6152 | tf_op jit(solution)/shard_map/ppermute | solution.py:19
  59.9 8.4 %collective-permute-start.14 = (f32[4,128,1]{2,1,0:T(8,128)S(1)}, f32[4,128,1]{2,1,0:T(8,128)S(1)}, u32[]{:S(2)}, u32[]{:S(2)}) collective-permute-start(f32[4,128,1]{2,1,0:T(8,128)S(1)} %slice.209), channel_id=1, source_target_pairs={{1,0},{2,1},{3,2},{4,3},{5,4},{6,5},{7,6},{9,8},{10,9},{11,10},{12... | collective-permute-start | bytes 6152 | tf_op jit(solution)/shard_map/ppermute | solution.py:19
  62.1 6.3 %collective-permute-start.13 = (f32[4,1,256]{2,1,0:T(1,128)S(1)}, f32[4,1,256]{2,1,0:T(1,128)S(1)}, u32[]{:S(2)}, u32[]{:S(2)}) collective-permute-start(f32[4,1,256]{2,1,0:T(1,128)S(1)} %slice.206), channel_id=1, source_target_pairs={{8,0},{16,8},{24,16},{32,24},{40,32},{48,40},{56,48},{64,56},{72,6... | collective-permute-start | bytes 12296 | tf_op jit(solution)/shard_map/ppermute | solution.py:19
  63.4 5.7 %collective-permute-start.12 = (f32[1,128,256]{2,1,0:T(8,128)S(1)}, f32[1,128,256]{2,1,0:T(8,128)S(1)}, u32[]{:S(2)}, u32[]{:S(2)}) collective-permute-start(f32[1,128,256]{2,1,0:T(8,128)S(1)} %slice.203), channel_id=1, source_target_pairs={{128,0},{256,128},{384,256},{129,1},{257,129},{385,257},{130,2},{2... | collective-permute-start | bytes 393224 | tf_op jit(solution)/shard_map/ppermute | solution.py:19
  70.0 16.3 %collective-permute-start.15 = (f32[1,128,256]{2,1,0:T(8,128)S(1)}, f32[1,128,256]{2,1,0:T(8,128)S(1)}, u32[]{:S(2)}, u32[]{:S(2)}) collective-permute-start(f32[1,128,256]{2,1,0:T(8,128)S(1)} %slice.210), channel_id=1, source_target_pairs={{0,128},{128,256},{256,384},{1,129},{129,257},{257,385},{2,130},{1... | collective-permute-start | bytes 393224 | tf_op jit(solution)/shard_map/ppermute | solution.py:19
  71.7 14.7 %collective-permute-start.16 = (f32[4,1,256]{2,1,0:T(1,128)S(1)}, f32[4,1,256]{2,1,0:T(1,128)S(1)}, u32[]{:S(2)}, u32[]{:S(2)}) collective-permute-start(f32[4,1,256]{2,1,0:T(1,128)S(1)} %slice.212), channel_id=1, source_target_pairs={{0,8},{8,16},{16,24},{24,32},{32,40},{40,48},{48,56},{56,64},{64,7... | collective-permute-start | bytes 12296 | tf_op jit(solution)/shard_map/ppermute | solution.py:19
  76.3 10.0 %collective-permute-start.17 = (f32[4,128,1]{2,1,0:T(8,128)S(1)}, f32[4,128,1]{2,1,0:T(8,128)S(1)}, u32[]{:S(2)}, u32[]{:S(2)}) collective-permute-start(f32[4,128,1]{2,1,0:T(8,128)S(1)} %slice.214), channel_id=1, source_target_pairs={{0,1},{1,2},{2,3},{3,4},{4,5},{5,6},{6,7},{8,9},{9,10},{10,11},{11... | collective-permute-start | bytes 6152 | tf_op jit(solution)/shard_map/ppermute | solution.py:19
where the time goes:
time: 154 us
  blocking collectives  60 us (39%)
  starting transfers between devices  54 us (35%)
  waiting for transfers between devices  23.6 us (15%)
  other arithmetic  12.5 us (8%)
  local copies, waits for them, and re-layouts  2.43 us (2%)
    psum x4, blocking collectives, one_axis_at_a_time(): value = lax.psum(value, axis)  60 us
    ppermute x18, starting transfers between devices, shifted(): return lax.ppermute(block, axis, route)  54 us
    ppermute x18, waiting for transfers between devices, shifted(): return lax.ppermute(block, axis, route)  23.6 us
    reduce_sum x2, other arithmetic, on_device(): local_sum = jnp.sum(term)  4.73 us
  transfers between devices with their start and end apart: 18, of which 9 were waited for; matrix products, arithmetic and copies ran while one was open for 1% of the time, Pallas kernels for 0%

commit v1 on v0

v1 whole, which is shorter than its diff:
```python
import functools

import jax
import jax.numpy as jnp
from jax import lax
from jax.experimental import pallas as pl
from jax.experimental.pallas import tpu as pltpu
from jax.sharding import PartitionSpec as P

ITERS = 3
SIGMA = 0.28
TAU = 0.28
TINY = 1.1754943508222875e-38
MESH = pl.DeviceIdType.MESH
F32 = jnp.float32

GROUPS = 16

FRAME_UP, FRAME_DOWN = (1, 0, 0), (-1, 0, 0)
ROW_UP, ROW_DOWN = (0, 1, 0), (0, -1, 0)
COL_UP, COL_DOWN = (0, 0, 1), (0, 0, -1)
NEIGHBOURS = (
    FRAME_UP, FRAME_DOWN, ROW_UP, ROW_DOWN, COL_UP, COL_DOWN,
    (1, -1, 0), (-1, 1, 0), (1, 0, -1), (-1, 0, 1), (0, 1, -1), (0, -1, 1),
)

CHUNKS = ([(0, 16)], [(0, 16)], [(0, 16)])
DUAL_STEPS = ([(0, 16)], [(0, 16)], [(0, 16)])
PRIMAL_STEPS = ([[(0, 16)]], [[(0, 16)]], [[(0, 16)]])


def rows_of(group):
    return pl.ds(pl.multiple_of(8 + 8 * group, 8), 8)


def kernel(
    sizes, f_hbm, fid_hbm, out_hbm, gaps_ref,
    ub, p, gu, res, damp, inv_fid, fid, out_v, c0, c255, cn, cp, tcn, tcp, rcn, rcp, pc, part, plane, part2, line,
    load_sem, out_sem,
    fr_send, fr_recv, row_send, row_recv, col_send, col_recv, tr_send, tr_recv, tc_send, tc_recv, rc_send, rc_recv,
    ar_send, ar_recv,
):
    n_tm, n_row, n_col = sizes
    at = (lax.axis_index("tm"), lax.axis_index("row"), lax.axis_index("col"))

    def there(step):
        return dict(tm=at[0] + step[0], row=at[1] + step[1], col=at[2] + step[2])

    def exists(step):
        found = None
        for pos, size, move in zip(at, sizes, step):
            if move:
                ok = pos < size - 1 if move > 0 else pos > 0
                found = ok if found is None else jnp.logical_and(found, ok)
        return found

    lane = lax.broadcasted_iota(jnp.int32, (8, 128), 1)
    sublane = lax.broadcasted_iota(jnp.int32, (8, 128), 0)
    first_lane, last_lane = lane == 0, lane == 127
    first_row, first_col, first_tm = at[1] == 0, at[2] == 0, at[0] == 0
    last_row, last_col, last_tm = at[1] == n_row - 1, at[2] == n_col - 1, at[0] == n_tm - 1
    edge_lane = jnp.logical_and(last_lane, last_col)

    loads = []
    for h in range(2):
        cols = pl.ds(128 * h, 128)
        loads.append(pltpu.make_async_copy(f_hbm.at[:, :, cols], ub.at[0, 1:5, h, 8:136, :], load_sem.at[h]))
        loads.append(pltpu.make_async_copy(fid_hbm.at[:, :, cols], fid.at[:, h], load_sem.at[2 + h]))
    for load in (loads[0], loads[2], loads[1], loads[3]):
        load.start()

    barrier = pltpu.get_barrier_semaphore()
    arrivals = (n_tm * n_col - 1) + (n_row - 1)
    for step in NEIGHBOURS:
        ok = exists(step)

        @pl.when(ok)
        def _():
            pl.semaphore_signal(barrier, inc=1, device_id=there(step), device_id_type=MESH)

        arrivals = arrivals + ok.astype(jnp.int32)

    def plane_mate(j):
        return dict(tm=lax.rem(at[0] + j // n_col, n_tm), row=at[1], col=lax.rem(at[2] + lax.rem(j, n_col), n_col))

    def line_mate(j):
        return dict(tm=at[0], row=lax.rem(at[1] + j, n_row), col=at[2])

    @pl.loop(1, n_tm * n_col)
    def _(j):
        pl.semaphore_signal(barrier, inc=1, device_id=plane_mate(j), device_id_type=MESH)

    @pl.loop(1, n_row)
    def _(j):
        pl.semaphore_signal(barrier, inc=1, device_id=line_mate(j), device_id_type=MESH)

    zero = jnp.zeros((8, 128), F32)
    p[...] = jnp.zeros_like(p)

    def remote(src, dst, send, recv, step):
        return pltpu.make_async_remote_copy(
            src_ref=src, dst_ref=dst, send_sem=send, recv_sem=recv, device_id=there(step), device_id_type=MESH
        )

    def frame_copies(k, c):
        g0, g1 = CHUNKS[k][c]
        out = []
        rows = pl.ds(8 + 8 * g0, 8 * (g1 - g0))
        for i, (step, src, dst) in enumerate(((FRAME_DOWN, 1, 5), (FRAME_UP, 4, 0))):
            out.append((step, remote(
                ub.at[k, src, :, rows, :], ub.at[k, dst, :, rows, :], fr_send.at[k, c, i], fr_recv.at[k, c, i], step)))
        return out

    def row_copies(k):
        out = []
        low, high = pl.ds(8, 8), pl.ds(128, 8)
        ghost_low, ghost_high = pl.ds(0, 8), pl.ds(136, 8)
        for i, (step, src, dst) in enumerate(((ROW_DOWN, low, ghost_high), (ROW_UP, high, ghost_low))):
            out.append((step, remote(
                ub.at[k, 1:5, :, src, :], ub.at[k, 1:5, :, dst, :], row_send.at[k, i], row_recv.at[k, i], step)))
        out.append(((1, -1, 0), remote(
            ub.at[k, 4, :, low, :], ub.at[k, 0, :, ghost_high, :], tr_send.at[k, 0], tr_recv.at[k, 0], (1, -1, 0))))
        out.append(((-1, 1, 0), remote(
            ub.at[k, 1, :, high, :], ub.at[k, 5, :, ghost_low, :], tr_send.at[k, 1], tr_recv.at[k, 1], (-1, 1, 0))))
        return out

    def col_copies(k, c):
        return [
            (COL_DOWN, remote(c0.at[k, c], cn.at[k, c], col_send.at[k, c, 0], col_recv.at[k, c, 0], COL_DOWN)),
            (COL_UP, remote(c255.at[k, c], cp.at[k, c], col_send.at[k, c, 1], col_recv.at[k, c, 1], COL_UP)),
            ((1, 0, -1), remote(c0.at[k, c], tcn.at[k, c], tc_send.at[k, c, 0], tc_recv.at[k, c, 0], (1, 0, -1))),
            ((-1, 0, 1), remote(c255.at[k, c], tcp.at[k, c], tc_send.at[k, c, 1], tc_recv.at[k, c, 1], (-1, 0, 1))),
        ]

    def corner_copies(k):
        c = len(CHUNKS[k]) - 1
        return [
            ((0, 1, -1), remote(c0.at[k, c], rcn.at[k], rc_send.at[k, 0], rc_recv.at[k, 0], (0, 1, -1))),
            ((0, -1, 1), remote(c255.at[k, c], rcp.at[k], rc_send.at[k, 1], rc_recv.at[k, 1], (0, -1, 1))),
        ]

    def start(copies):
        for step, copy in copies:
            @pl.when(exists(step))
            def _():
                copy.start()

    def wait_sent(copies):
        for step, copy in copies:
            @pl.when(exists(step))
            def _():
                copy.wait_send()

    def wait_received(copies):
        for step, copy in copies:
            @pl.when(exists(tuple(-s for s in step)))
            def _():
                copy.wait_recv()

    def all_copies(k):
        out = row_copies(k) + corner_copies(k)
        for c in range(len(CHUNKS[k])):
            out += frame_copies(k, c) + col_copies(k, c)
        return out

    def packed_at(t, g):
        return (t - 1) * 16 + g

    def packed(x0, x1, t, g, held):
        i = packed_at(t, g)
        here = lane == i
        return (
            jnp.where(here, pltpu.roll(x0, i, 1), held[0]),
            jnp.where(here, pltpu.roll(x1, i + 1, 1), held[1]),
        )

    def pack_first():
        def body(g, held):
            for t in range(1, 5):
                held = packed(ub[0, t, 0, rows_of(g), :], ub[0, t, 1, rows_of(g), :], t, g, held)
            return held

        return lax.fori_loop(0, GROUPS, body, (zero, zero))

    def project(k, m, g):
        if k == 0:
            square = g[0] * g[0] + g[1] * g[1] + g[2] * g[2]
            root = lax.rsqrt(jnp.maximum(square, TINY))
            scale = jnp.minimum(SIGMA, root)
            return [g[d] * scale for d in range(3)], square * root
        square = m[0] * m[0] + m[1] * m[1] + m[2] * m[2]
        scale = lax.rsqrt(jnp.maximum(square, 1.0))
        return [m[d] * scale for d in range(3)], None

    def dual_group(k, rows, below, frames, ghost_of, total):
        x = [[ub[k, t, h, rows, :] for h in range(2)] for t in range(frames[0], 6)]
        for t in frames:
            here, later = x[t - frames[0]], x[t - frames[0] + 1]
            rolled = [pltpu.roll(here[h], 127, 1) for h in range(2)]
            after = [
                jnp.where(last_lane, rolled[1], rolled[0]),
                jnp.where(edge_lane, here[1], jnp.where(last_lane, ghost_of(t), rolled[1])),
            ]
            for h in range(2):
                g = [later[h] - here[h], ub[k, t, h, below, :] - here[h], after[h] - here[h]]
                m = None if k == 0 else [p[d, t, h, rows, :] + SIGMA * g[d] for d in range(3)]
                new, length = project(k, m, g)
                for d in range(3):
                    p[d, t, h, rows, :] = new[d]
                if total is None or t == 0:
                    continue
                if k == 0:
                    for d in range(3):
                        gu[d, t - 1, h, pl.ds(rows.start - 8, 8), :] = g[d]
                    total = total + length
                else:
                    own = pl.ds(rows.start - 8, 8)
                    if k == 1:
                        s = [g[d] + gu[d, t - 1, h, own, :] for d in range(3)]
                        for d in range(3):
                            gu[d, t - 1, h, own, :] = s[d]
                    else:
                        s = [g[d] + 0.5 * gu[d, t - 1, h, own, :] for d in range(3)]
                    square = s[0] * s[0] + s[1] * s[1] + s[2] * s[2]
                    total = total + square * lax.rsqrt(jnp.maximum(square, TINY))
        return total

    def dual_range(k, c, g0, g1, total):
        def body(g, total):
            rows = rows_of(g)
            nexts, frame_nexts = cn[k, c], tcn[k, c]

            def ghost_of(t):
                if t == 0:
                    return pltpu.roll(frame_nexts, 127 - packed_at(4, g), 1)
                return pltpu.roll(nexts, 127 - packed_at(t, g), 1)

            return dual_group(k, rows, pl.ds(rows.start + 1, 8), range(5), ghost_of, total)

        return lax.fori_loop(g0, g1, body, total)

    def dual_above(k):
        @pl.when(jnp.logical_not(first_row))
        def _():
            nexts = rcn[k]
            dual_group(
                k, pl.ds(0, 8), pl.ds(1, 8), range(1, 5),
                lambda t: pltpu.roll(nexts, 127 - packed_at(t, 15), 1), None,
            )

    def dual_left(k, c):
        here, below_left, later_left = cp[k, c], rcp[k], tcp[k, c]
        later = jnp.where(lane >= 48, pltpu.roll(later_left, 48, 1), pltpu.roll(here, 112, 1))
        later = jnp.where(jnp.logical_and(lane >= 48, last_tm), here, later)
        last_group = jnp.bitwise_and(lane, 15) == 15
        follow = jnp.where(last_group, pltpu.roll(below_left, 15, 1), pltpu.roll(here, 127, 1))
        below = jnp.where(sublane == 7, pltpu.roll(follow, 7, 0), pltpu.roll(here, 7, 0))
        bottom = jnp.logical_and(jnp.logical_and(sublane == 7, last_group), last_row)
        below = jnp.where(bottom, here, below)
        g = [later - here, below - here, c0[k, c] - here]
        m = None if k == 0 else [pc[k, d] + SIGMA * g[d] for d in range(3)]
        new, _ = project(k, m, g)
        for d in range(3):
            pc[k + 1, d] = new[d]
        pc[k + 1, 3] = jnp.where(first_col, 0.0, new[2])

    def primal_range(k, g0, g1, carry):
        def body(g, carry):
            total, held = carry
            rows = rows_of(g)
            own = pl.ds(rows.start - 8, 8)
            before_rows = pl.ds(rows.start - 1, 8)
            left = pc[k + 1, 3]
            for t in range(1, 5):
                q = [p[2, t, h, rows, :] for h in range(2)]
                rolled = [pltpu.roll(q[h], 1, 1) for h in range(2)]
                ghost = pltpu.roll(left, 128 - packed_at(t, g), 1)
                before = [jnp.where(first_lane, ghost, rolled[0]), jnp.where(first_lane, rolled[0], rolled[1])]
                bars = []
                for h in range(2):
                    e = (
                        (p[0, t, h, rows, :] - p[0, t - 1, h, rows, :])
                        + (p[1, t, h, rows, :] - p[1, t, h, before_rows, :])
                        + (q[h] - before[h])
                    )
                    f = ub[0, t, h, rows, :]
                    scale = damp[t - 1, h, own, :]
                    total = total + (e * e * inv_fid[t - 1, h, own, :] + f * e)
                    if k == 0:
                        new = scale * (TAU * e)
                        bar = f + 2.0 * new
                    else:
                        old = res[t - 1, h, own, :]
                        total = total + old * old * fid[t - 1, h, own, :]
                        new = scale * (old + TAU * e)
                        bar = f + (2.0 * new - old)
                    if k < ITERS - 1:
                        res[t - 1, h, own, :] = new
                        ub[k + 1, t, h, rows, :] = bar
                        bars.append(bar)
                    else:
                        out_v[t - 1, h, own, :] = f + new
                if k < ITERS - 1:
                    held = packed(bars[0], bars[1], t, g, held)
            return total, held

        return lax.fori_loop(g0, g1, body, carry)

    def weights():
        for h in range(2):
            loads[2 * h + 1].wait()

        @pl.loop(0, GROUPS)
        def _(g):
            own = pl.ds(pl.multiple_of(8 * g, 8), 8)
            for t in range(4):
                for h in range(2):
                    lam = fid[t, h, own, :]
                    damp[t, h, own, :] = 1.0 / (1.0 + TAU * lam)
                    inv_fid[t, h, own, :] = 0.5 / lam
                    fid[t, h, own, :] = 0.5 * lam

    def send(k, c, held):
        c0[k, c], c255[k, c] = held
        start(frame_copies(k, c) + col_copies(k, c))
        if c == len(CHUNKS[k]) - 1:
            start(row_copies(k) + corner_copies(k))

    for h in range(2):
        loads[2 * h].wait()
    held = pack_first()
    pl.semaphore_wait(barrier, arrivals)
    for c in range(len(CHUNKS[0])):
        send(0, c, held)
    weights()

    sums = []
    for k in range(ITERS):
        length, total, held = zero, zero, (zero, zero)
        for c in range(len(CHUNKS[k])):
            if c == 0:
                wait_received(row_copies(k) + corner_copies(k))
            wait_received(frame_copies(k, c) + col_copies(k, c))

            @pl.when(last_tm)
            def _():
                ub[k, 5] = ub[k, 4]

            @pl.when(last_row)
            def _():
                for t in range(5):
                    for h in range(2):
                        ub[k, t, h, 136:137, :] = ub[k, t, h, 135:136, :]

            dual_left(k, c)
            if c == 0:
                dual_above(k)
            length = dual_range(k, c, *DUAL_STEPS[k][c], length)

            @pl.when(first_tm)
            def _():
                p[0, 0] = jnp.zeros_like(p[0, 0])

            for span in PRIMAL_STEPS[k][c]:
                total, held = primal_range(k, *span, (total, held))
            if k < ITERS - 1:
                send(k + 1, c, held)
        sums.append(total + (1.0 if k == 0 else 0.5) * length)

    puts = [
        pltpu.make_async_copy(out_v.at[:, h], out_hbm.at[:, :, pl.ds(128 * h, 128)], out_sem.at[h]) for h in range(2)
    ]
    for put in puts:
        put.start()

    row = jnp.zeros((1, 128), F32)
    row_lane = lax.broadcasted_iota(jnp.int32, (1, 128), 1)
    for k in range(ITERS):
        row = jnp.where(row_lane == k, jnp.sum(sums[k]), row)

    def exchange(mine, slots, me, count, mate, i, row):
        mine[0] = row
        slots[me] = row

        @pl.loop(1, count)
        def _(j):
            pltpu.make_async_remote_copy(
                src_ref=mine.at[0], dst_ref=slots.at[me], send_sem=ar_send.at[i], recv_sem=ar_recv.at[i],
                device_id=mate(j), device_id_type=MESH,
            ).start()

        landed = slots.at[pl.ds(0, count - 1)]
        pltpu.make_async_copy(landed, landed, ar_recv.at[i]).wait()
        got = slots[0]
        for j in range(1, count):
            got = got + slots[j]
        return got

    def drain(slots, count, i):
        landed = slots.at[pl.ds(0, count - 1)]
        pltpu.make_async_copy(landed, landed, ar_send.at[i]).wait()

    row = exchange(part, plane, at[0] * n_col + at[2], n_tm * n_col, plane_mate, 0, row)
    row = exchange(part2, line, at[1], n_row, line_mate, 1, row)
    cells = float(4 * 128 * 256) * float(n_tm * n_row * n_col)
    gaps_ref[...] = row * (1.0 / cells)

    for k in range(ITERS):
        wait_sent(all_copies(k))
    drain(plane, n_tm * n_col, 0)
    drain(line, n_row, 1)
    for put in puts:
        put.wait()


def on_device(sizes, noisy_video, fidelity):
    n_chunks = max(len(c) for c in CHUNKS)
    dma = pltpu.SemaphoreType.DMA
    vmem = lambda *shape: pltpu.VMEM(shape, F32)
    n_plane, n_row = sizes[0] * sizes[2], sizes[1]
    out, gaps = pl.pallas_call(
        functools.partial(kernel, sizes),
        out_shape=(jax.ShapeDtypeStruct(noisy_video.shape, F32), jax.ShapeDtypeStruct((1, 128), F32)),
        in_specs=[pl.BlockSpec(memory_space=pl.ANY)] * 2,
        out_specs=(pl.BlockSpec(memory_space=pl.ANY), pl.BlockSpec(memory_space=pltpu.VMEM)),
        scratch_shapes=[
            vmem(3, 6, 2, 144, 128),
            vmem(3, 5, 2, 136, 128),
            vmem(3, 4, 2, 128, 128),
            vmem(4, 2, 128, 128),
            vmem(4, 2, 128, 128),
            vmem(4, 2, 128, 128),
            vmem(4, 2, 128, 128),
            vmem(4, 2, 128, 128),
            vmem(3, n_chunks, 8, 128),
            vmem(3, n_chunks, 8, 128),
            vmem(3, n_chunks, 8, 128),
            vmem(3, n_chunks, 8, 128),
            vmem(3, n_chunks, 8, 128),
            vmem(3, n_chunks, 8, 128),
            vmem(3, 8, 128),
            vmem(3, 8, 128),
            vmem(4, 4, 8, 128),
            vmem(1, 1, 128),
            vmem(n_plane, 1, 128),
            vmem(1, 1, 128),
            vmem(n_row, 1, 128),
            dma((4,)),
            dma((2,)),
            dma((3, n_chunks, 2)), dma((3, n_chunks, 2)),
            dma((3, 2)), dma((3, 2)),
            dma((3, n_chunks, 2)), dma((3, n_chunks, 2)),
            dma((3, 2)), dma((3, 2)),
            dma((3, n_chunks, 2)), dma((3, n_chunks, 2)),
            dma((3, 2)), dma((3, 2)),
            dma((2,)), dma((2,)),
        ],
        compiler_params=pltpu.CompilerParams(collective_id=0, has_side_effects=True),
    )(noisy_video, fidelity)
    return out, gaps[0, :3]


def solution(mesh):
    sizes = (mesh.shape["tm"], mesh.shape["row"], mesh.shape["col"])
    placed = P("tm", "row", "col")
    return jax.shard_map(
        functools.partial(on_device, sizes),
        mesh=mesh,
        in_specs=(placed, placed),
        out_specs=(placed, P()),
        check_vma=False,
    )
```

time: 154 us -> 61.1 us (0.40)
  blocking collectives: 60 us -> 0 us
  Pallas kernels: 0 us -> 57.2 us
  starting transfers between devices: 54 us -> 0 us
  waiting for transfers between devices: 23.6 us -> 0 us
  other arithmetic: 12.5 us -> 0 us
    psum x4 -> x0, blocking collectives: 60 us -> none  [one_axis_at_a_time(): value = lax.psum(value, axis)]
    pallas_call x0 -> x1, Pallas kernels: none -> 57.2 us  [on_device(): pl.pallas_call(functools.partial(kernel, sizes), out_shape=(jax.ShapeDtyp...]
    ppermute x18 -> x0, starting transfers between devices: 54 us -> none  [shifted(): return lax.ppermute(block, axis, route)]
    ppermute x18 -> x0, waiting for transfers between devices: 23.6 us -> none  [shifted(): return lax.ppermute(block, axis, route)]
    reduce_sum x2 -> x0, other arithmetic: 4.73 us -> none  [on_device(): local_sum = jnp.sum(term)]
    div x7 -> x0, other arithmetic: 4.62 us -> none  [the longest x1 2.12 us: on_device(): (field + tau_step * diverge + tau_step * fidelity * noisy_video) / (1.0 +...]
    unnamed x4 -> x3, local copies, waits for them, and re-layouts: 0.01 us -> 2.53 us
    slice x30 -> x0, local copies, waits for them, and re-layouts: 2.42 us -> none  [the longest x3 1.07 us: on_device(): ghost_cols = shifted(ubar_field[:, :, 0:1], COL, -1)]
  transfers between devices with their start and end apart: 18 -> 0, of which waited for: 9 -> 0; matrix products, arithmetic and copies ran while one was open for 1% -> 0% of each run, Pallas kernels for 0% -> 0%
where the time goes in v1:
time: 61.1 us; the launch traced here: 60.9 us
  Pallas kernels  57.2 us (94%)
  local copies, waits for them, and re-layouts  3.04 us (5%)
  between operations  0.65 us (1%)
    pallas_call x1, Pallas kernels, on_device(): pl.pallas_call(functools.partial(kernel, sizes), out_shape=(jax.ShapeDtyp...  57.2 us
    unnamed x3, local copies, waits for them, and re-layouts  2.53 us

profile of v1, /device:TPU:1, one launch (start us, length us, event | category | flops | bytes accessed | tf_op | source)
XLA Modules:
  0.0 60.9 jit_solution(3332570816947158378)
XLA Ops:
  0.6 57.2 %shard_map.41 = (f32[4,128,256]{2,1,0:T(8,128)}, f32[1,128]{1,0:T(1,128)}) custom-call(f32[4,128,256]{2,1,0:T(8,128)} %f_hbm.1, f32[4,128,256]{2,1,0:T(8,128)} %fid_hbm.1), custom_call_target="tpu_custom_call" | custom-call | tf_op jit(solution)/shard_map/pallas_call | solution.py:421
  57.9 0.0 copy-start
  57.9 0.7 %copy-done = f32[1,128]{1,0:T(1,128)S(1)} copy-done((f32[1,128]{1,0:T(1,128)S(1)}, f32[1,128]{1,0:T(1,128)}, u32[]{:S(2)}) %copy-start) | copy-done | bytes 536
  58.5 0.5 slice_bitcast_fusion
  59.1 1.9 %copy.5 = f32[4,128,256]{2,1,0:T(8,128)} copy(f32[4,128,256]{2,1,0:T(8,128)} %get-tuple-element.8) | data formatting | bytes 1048576
Async XLA Ops:
  57.9 0.7 %copy-start = (f32[1,128]{1,0:T(1,128)S(1)}, f32[1,128]{1,0:T(1,128)}, u32[]{:S(2)}) copy-start(f32[1,128]{1,0:T(1,128)} %get-tuple-element.5) | copy-start | bytes 1540

commit v2 on v1

--- a/solution.py
+++ b/solution.py
@@ -1,4 +1,5 @@
 import functools
+from itertools import zip_longest
 
 import jax
 import jax.numpy as jnp
@@ -29,16 +30,38 @@
 PRIMAL_STEPS = ([[(0, 16)]], [[(0, 16)]], [[(0, 16)]])
 
 
+UNROLL = 4
+PACK_UNROLL = 8
+
+
+def grouped(g0, g1, body, carry, unroll):
+    steps = (g1 - g0) // unroll
+
+    def step(i, carry):
+        for u in range(unroll):
+            carry = body(g0 + i * unroll + u, carry)
+        return carry
+
+    if steps > 1:
+        carry = lax.fori_loop(0, steps, step, carry)
+    elif steps == 1:
+        carry = step(0, carry)
+    for g in range(g0 + steps * unroll, g1):
+        carry = body(g, carry)
+    return carry
+
+
 def rows_of(group):
-    return pl.ds(pl.multiple_of(8 + 8 * group, 8), 8)
+    start = 8 + 8 * group
+    return pl.ds(start if isinstance(start, int) else pl.multiple_of(start, 8), 8)
 
 
 def kernel(
     sizes, f_hbm, fid_hbm, out_hbm, gaps_ref,
-    ub, p, gu, res, damp, inv_fid, fid, out_v, c0, c255, cn, cp, tcn, tcp, rcn, rcp, pc, part, plane, part2, line,
+    ub, p, gu, res, damp, inv_fid, fid, out_v, c0, c255, cn, cp, tcn, tcp, rcn, rcp, pc, part, by_col, by_tm, by_row,
     load_sem, out_sem,
     fr_send, fr_recv, row_send, row_recv, col_send, col_recv, tr_send, tr_recv, tc_send, tc_recv, rc_send, rc_recv,
-    ar_send, ar_recv,
+    ar_send, ar_recv, token_sem,
 ):
     n_tm, n_row, n_col = sizes
     at = (lax.axis_index("tm"), lax.axis_index("row"), lax.axis_index("col"))
@@ -69,30 +92,49 @@
     for load in (loads[0], loads[2], loads[1], loads[3]):
         load.start()
 
+    def ring(**moves):
+        out = {}
+        for name, pos, size in zip(("tm", "row", "col"), at, sizes):
+            out[name] = lax.rem(pos + (moves.get(name, 0) + size), size)
+        return out
+
     barrier = pltpu.get_barrier_semaphore()
-    arrivals = (n_tm * n_col - 1) + (n_row - 1)
-    for step in NEIGHBOURS:
-        ok = exists(step)
+    arrivals = 0
+    for move in NEIGHBOURS:
+        if sum(map(abs, move)) == 1:
+            pl.semaphore_signal(
+                barrier, inc=1, device_id=ring(tm=move[0], row=move[1], col=move[2]), device_id_type=MESH)
+            arrivals = arrivals + 1
+            continue
+        ok = exists(move)
 
         @pl.when(ok)
         def _():
-            pl.semaphore_signal(barrier, inc=1, device_id=there(step), device_id_type=MESH)
+            pl.semaphore_signal(barrier, inc=1, device_id=there(move), device_id_type=MESH)
 
         arrivals = arrivals + ok.astype(jnp.int32)
 
-    def plane_mate(j):
-        return dict(tm=lax.rem(at[0] + j // n_col, n_tm), row=at[1], col=lax.rem(at[2] + lax.rem(j, n_col), n_col))
-
-    def line_mate(j):
-        return dict(tm=at[0], row=lax.rem(at[1] + j, n_row), col=at[2])
-
-    @pl.loop(1, n_tm * n_col)
-    def _(j):
-        pl.semaphore_signal(barrier, inc=1, device_id=plane_mate(j), device_id_type=MESH)
-
-    @pl.loop(1, n_row)
-    def _(j):
-        pl.semaphore_signal(barrier, inc=1, device_id=line_mate(j), device_id_type=MESH)
+    def tokens(name, count):
+        reach, out = 1, []
+        while 2 * reach < count:
+            out.append((name, reach))
+            reach *= 2
+        return out
+
+    rounds = list(zip_longest(tokens("row", n_row), tokens("col", n_col), tokens("tm", n_tm)))
+
+    def tell(i):
+        for j, token in enumerate(rounds[i] if i < len(rounds) else ()):
+            if token:
+                name, reach = token
+                for d in (reach, -reach):
+                    pl.semaphore_signal(
+                        token_sem.at[i, j], inc=1, device_id=ring(**{name: d}), device_id_type=MESH)
+
+    def hear(i):
+        for j, token in enumerate(rounds[i] if i < len(rounds) else ()):
+            if token:
+                pl.semaphore_wait(token_sem.at[i, j], 2)
 
     zero = jnp.zeros((8, 128), F32)
     p[...] = jnp.zeros_like(p)
@@ -174,13 +216,13 @@
             jnp.where(here, pltpu.roll(x1, i + 1, 1), held[1]),
         )
 
-    def pack_first():
+    def pack(k, g0, g1, held):
         def body(g, held):
             for t in range(1, 5):
-                held = packed(ub[0, t, 0, rows_of(g), :], ub[0, t, 1, rows_of(g), :], t, g, held)
+                held = packed(ub[k, t, 0, rows_of(g), :], ub[k, t, 1, rows_of(g), :], t, g, held)
             return held
 
-        return lax.fori_loop(0, GROUPS, body, (zero, zero))
+        return grouped(g0, g1, body, held, PACK_UNROLL)
 
     def project(k, m, g):
         if k == 0:
@@ -237,7 +279,7 @@
 
             return dual_group(k, rows, pl.ds(rows.start + 1, 8), range(5), ghost_of, total)
 
-        return lax.fori_loop(g0, g1, body, total)
+        return grouped(g0, g1, body, total, UNROLL)
 
     def dual_above(k):
         @pl.when(jnp.logical_not(first_row))
@@ -264,9 +306,8 @@
             pc[k + 1, d] = new[d]
         pc[k + 1, 3] = jnp.where(first_col, 0.0, new[2])
 
-    def primal_range(k, g0, g1, carry):
-        def body(g, carry):
-            total, held = carry
+    def primal_range(k, g0, g1, total):
+        def body(g, total):
             rows = rows_of(g)
             own = pl.ds(rows.start - 8, 8)
             before_rows = pl.ds(rows.start - 1, 8)
@@ -276,7 +317,6 @@
                 rolled = [pltpu.roll(q[h], 1, 1) for h in range(2)]
                 ghost = pltpu.roll(left, 128 - packed_at(t, g), 1)
                 before = [jnp.where(first_lane, ghost, rolled[0]), jnp.where(first_lane, rolled[0], rolled[1])]
-                bars = []
                 for h in range(2):
                     e = (
                         (p[0, t, h, rows, :] - p[0, t - 1, h, rows, :])
@@ -297,14 +337,11 @@
                     if k < ITERS - 1:
                         res[t - 1, h, own, :] = new
                         ub[k + 1, t, h, rows, :] = bar
-                        bars.append(bar)
                     else:
                         out_v[t - 1, h, own, :] = f + new
-                if k < ITERS - 1:
-                    held = packed(bars[0], bars[1], t, g, held)
-            return total, held
-
-        return lax.fori_loop(g0, g1, body, carry)
+            return total
+
+        return grouped(g0, g1, body, total, UNROLL)
 
     def weights():
         for h in range(2):
@@ -328,11 +365,15 @@
 
     for h in range(2):
         loads[2 * h].wait()
-    held = pack_first()
+    held = pack(0, 0, GROUPS, (zero, zero))
     pl.semaphore_wait(barrier, arrivals)
+    tell(0)
     for c in range(len(CHUNKS[0])):
         send(0, c, held)
     weights()
+
+    hear(0)
+    tell(1)
 
     sums = []
     for k in range(ITERS):
@@ -352,6 +393,9 @@
                     for h in range(2):
                         ub[k, t, h, 136:137, :] = ub[k, t, h, 135:136, :]
 
+            if c == 0:
+                hear(k + 1)
+                tell(k + 2)
             dual_left(k, c)
             if c == 0:
                 dual_above(k)
@@ -362,7 +406,9 @@
                 p[0, 0] = jnp.zeros_like(p[0, 0])
 
             for span in PRIMAL_STEPS[k][c]:
-                total, held = primal_range(k, *span, (total, held))
+                total = primal_range(k, *span, total)
+                if k < ITERS - 1:
+                    held = pack(k + 1, *span, held)
             if k < ITERS - 1:
                 send(k + 1, c, held)
         sums.append(total + (1.0 if k == 0 else 0.5) * length)
@@ -378,15 +424,15 @@
     for k in range(ITERS):
         row = jnp.where(row_lane == k, jnp.sum(sums[k]), row)
 
-    def exchange(mine, slots, me, count, mate, i, row):
-        mine[0] = row
+    def exchange(mine, slots, me, count, name, i, row):
+        mine[...] = row
         slots[me] = row
 
         @pl.loop(1, count)
         def _(j):
             pltpu.make_async_remote_copy(
-                src_ref=mine.at[0], dst_ref=slots.at[me], send_sem=ar_send.at[i], recv_sem=ar_recv.at[i],
-                device_id=mate(j), device_id_type=MESH,
+                src_ref=mine, dst_ref=slots.at[me], send_sem=ar_send.at[i], recv_sem=ar_recv.at[i],
+                device_id=ring(**{name: j}), device_id_type=MESH,
             ).start()
 
         landed = slots.at[pl.ds(0, count - 1)]
@@ -400,15 +446,17 @@
         landed = slots.at[pl.ds(0, count - 1)]
         pltpu.make_async_copy(landed, landed, ar_send.at[i]).wait()
 
-    row = exchange(part, plane, at[0] * n_col + at[2], n_tm * n_col, plane_mate, 0, row)
-    row = exchange(part2, line, at[1], n_row, line_mate, 1, row)
+    row = exchange(part.at[0], by_col, at[2], n_col, "col", 0, row)
+    row = exchange(part.at[1], by_tm, at[0], n_tm, "tm", 1, row)
+    row = exchange(part.at[2], by_row, at[1], n_row, "row", 2, row)
     cells = float(4 * 128 * 256) * float(n_tm * n_row * n_col)
     gaps_ref[...] = row * (1.0 / cells)
 
     for k in range(ITERS):
         wait_sent(all_copies(k))
-    drain(plane, n_tm * n_col, 0)
-    drain(line, n_row, 1)
+    drain(by_col, n_col, 0)
+    drain(by_tm, n_tm, 1)
+    drain(by_row, n_row, 2)
     for put in puts:
         put.wait()
 
@@ -417,7 +465,6 @@
     n_chunks = max(len(c) for c in CHUNKS)
     dma = pltpu.SemaphoreType.DMA
     vmem = lambda *shape: pltpu.VMEM(shape, F32)
-    n_plane, n_row = sizes[0] * sizes[2], sizes[1]
     out, gaps = pl.pallas_call(
         functools.partial(kernel, sizes),
         out_shape=(jax.ShapeDtypeStruct(noisy_video.shape, F32), jax.ShapeDtypeStruct((1, 128), F32)),
@@ -441,10 +488,10 @@
             vmem(3, 8, 128),
             vmem(3, 8, 128),
             vmem(4, 4, 8, 128),
-            vmem(1, 1, 128),
-            vmem(n_plane, 1, 128),
-            vmem(1, 1, 128),
-            vmem(n_row, 1, 128),
+            vmem(3, 1, 128),
+            vmem(sizes[2], 1, 128),
+            vmem(sizes[0], 1, 128),
+            vmem(sizes[1], 1, 128),
             dma((4,)),
             dma((2,)),
             dma((3, n_chunks, 2)), dma((3, n_chunks, 2)),
@@ -453,7 +500,8 @@
             dma((3, 2)), dma((3, 2)),
             dma((3, n_chunks, 2)), dma((3, n_chunks, 2)),
             dma((3, 2)), dma((3, 2)),
-            dma((2,)), dma((2,)),
+            dma((3,)), dma((3,)),
+            pltpu.SemaphoreType.REGULAR((4, 3)),
         ],
         compiler_params=pltpu.CompilerParams(collective_id=0, has_side_effects=True),
     )(noisy_video, fidelity)

time: 61.1 us -> 52.1 us (0.85)
  Pallas kernels: 57.2 us -> 48 us
    pallas_call x1, Pallas kernels: 57.2 us -> 48 us  [on_device(): pl.pallas_call(functools.partial(kernel, sizes), out_shape=(jax.ShapeDtyp...]
where the time goes in v2:
time: 52.1 us; the launch traced here: 51.7 us
  Pallas kernels  48 us (92%)
  local copies, waits for them, and re-layouts  3.04 us (6%)
  between operations  0.65 us (1%)
    pallas_call x1, Pallas kernels, on_device(): pl.pallas_call(functools.partial(kernel, sizes), out_shape=(jax.ShapeDtyp...  48 us
    unnamed x3, local copies, waits for them, and re-layouts  2.53 us

profile of v2, /device:TPU:1, one launch (start us, length us, event | category | flops | bytes accessed | tf_op | source)
XLA Modules:
  0.0 51.7 jit_solution(11559423017503734203)
XLA Ops:
  0.6 48.0 %shard_map.41 = (f32[4,128,256]{2,1,0:T(8,128)}, f32[1,128]{1,0:T(1,128)}) custom-call(f32[4,128,256]{2,1,0:T(8,128)} %f_hbm.1, f32[4,128,256]{2,1,0:T(8,128)} %fid_hbm.1), custom_call_target="tpu_custom_call" | custom-call | tf_op jit(solution)/shard_map/pallas_call | solution.py:468
  48.6 0.0 copy-start
  48.6 0.7 %copy-done = f32[1,128]{1,0:T(1,128)S(1)} copy-done((f32[1,128]{1,0:T(1,128)S(1)}, f32[1,128]{1,0:T(1,128)}, u32[]{:S(2)}) %copy-start) | copy-done | bytes 536
  49.3 0.5 slice_bitcast_fusion
  49.8 1.9 %copy.5 = f32[4,128,256]{2,1,0:T(8,128)} copy(f32[4,128,256]{2,1,0:T(8,128)} %get-tuple-element.8) | data formatting | bytes 1048576
Async XLA Ops:
  48.6 0.7 %copy-start = (f32[1,128]{1,0:T(1,128)S(1)}, f32[1,128]{1,0:T(1,128)}, u32[]{:S(2)}) copy-start(f32[1,128]{1,0:T(1,128)} %get-tuple-element.5) | copy-start | bytes 1540

commit v3 on v2

--- a/solution.py
+++ b/solution.py
@@ -25,13 +25,27 @@
     (1, -1, 0), (-1, 1, 0), (1, 0, -1), (-1, 0, 1), (0, 1, -1), (0, -1, 1),
 )
 
-CHUNKS = ([(0, 16)], [(0, 16)], [(0, 16)])
-DUAL_STEPS = ([(0, 16)], [(0, 16)], [(0, 16)])
-PRIMAL_STEPS = ([[(0, 16)]], [[(0, 16)]], [[(0, 16)]])
-
+CHUNKS = (
+    ([(0, 5)], [(5, 9)], [(9, 13)], [(13, 16)]),
+    ([(0, 4)], [(4, 8)], [(8, 12)], [(12, 16)]),
+    ([(1, 3)], [(3, 7)], [(7, 11)], [(11, 16), (0, 1)]),
+)
+DUAL_STEPS = (
+    ([(0, 4)], [(4, 8)], [(8, 12)], [(12, 16)]),
+    ([(0, 3)], [(3, 7)], [(7, 11)], [(11, 16)]),
+    ([(1, 2)], [(2, 6)], [(6, 10)], [(10, 16), (0, 1)]),
+)
+PRIMAL_STEPS = (
+    ([(0, 4)], [(4, 8)], [(8, 12)], [(12, 16)]),
+    ([(1, 3)], [(3, 7)], [(7, 11)], [(11, 16), (0, 1)]),
+    ([], [(2, 6)], [(6, 10)], [(10, 16), (0, 2)]),
+)
+STEPS = 4
+ABOVE_STEP = (0, 3, 3)
+LOW_CHUNK = (3, 0, 3)
 
 UNROLL = 4
-PACK_UNROLL = 8
+PACK_UNROLL = 5
 
 
 def grouped(g0, g1, body, carry, unroll):
@@ -57,9 +71,9 @@
 
 
 def kernel(
-    sizes, f_hbm, fid_hbm, out_hbm, gaps_ref,
-    ub, p, gu, res, damp, inv_fid, fid, out_v, c0, c255, cn, cp, tcn, tcp, rcn, rcp, pc, part, by_col, by_tm, by_row,
-    load_sem, out_sem,
+    sizes, f_hbm, fid_hbm, out_v, gaps_ref,
+    ub, p, gu, res, damp, inv_fid, fid, c0, c255, cn, cp, tcn, tcp, rcn, rcp, pc, part, by_col, by_tm, by_row,
+    load_sem,
     fr_send, fr_recv, row_send, row_recv, col_send, col_recv, tr_send, tr_recv, tc_send, tc_recv, rc_send, rc_recv,
     ar_send, ar_recv, token_sem,
 ):
@@ -84,12 +98,17 @@
     last_row, last_col, last_tm = at[1] == n_row - 1, at[2] == n_col - 1, at[0] == n_tm - 1
     edge_lane = jnp.logical_and(last_lane, last_col)
 
-    loads = []
+    frame_loads, fid_loads = {}, []
     for h in range(2):
         cols = pl.ds(128 * h, 128)
-        loads.append(pltpu.make_async_copy(f_hbm.at[:, :, cols], ub.at[0, 1:5, h, 8:136, :], load_sem.at[h]))
-        loads.append(pltpu.make_async_copy(fid_hbm.at[:, :, cols], fid.at[:, h], load_sem.at[2 + h]))
-    for load in (loads[0], loads[2], loads[1], loads[3]):
+        for t in range(4):
+            frame_loads[t, h] = pltpu.make_async_copy(
+                f_hbm.at[t, :, cols], ub.at[0, t + 1, h, 8:136, :], load_sem.at[t, h])
+        fid_loads.append(pltpu.make_async_copy(fid_hbm.at[:, :, cols], fid.at[:, h], load_sem.at[4, h]))
+    for t in (0, 3, 1, 2):
+        for h in range(2):
+            frame_loads[t, h].start()
+    for load in fid_loads:
         load.start()
 
     def ring(**moves):
@@ -137,7 +156,12 @@
                 pl.semaphore_wait(token_sem.at[i, j], 2)
 
     zero = jnp.zeros((8, 128), F32)
-    p[...] = jnp.zeros_like(p)
+
+    @pl.when(first_row)
+    def _():
+        for t in range(1, 5):
+            for h in range(2):
+                p[1, t, h, 0:8, :] = zero
 
     def remote(src, dst, send, recv, step):
         return pltpu.make_async_remote_copy(
@@ -145,26 +169,36 @@
         )
 
     def frame_copies(k, c):
-        g0, g1 = CHUNKS[k][c]
         out = []
-        rows = pl.ds(8 + 8 * g0, 8 * (g1 - g0))
-        for i, (step, src, dst) in enumerate(((FRAME_DOWN, 1, 5), (FRAME_UP, 4, 0))):
-            out.append((step, remote(
-                ub.at[k, src, :, rows, :], ub.at[k, dst, :, rows, :], fr_send.at[k, c, i], fr_recv.at[k, c, i], step)))
+        for i, (move, src, dst) in enumerate(((FRAME_DOWN, 1, 5), (FRAME_UP, 4, 0))):
+            for j, (g0, g1) in enumerate(CHUNKS[k][c]):
+                rows = pl.ds(8 + 8 * g0, 8 * (g1 - g0))
+                out.append((move, remote(
+                    ub.at[k, src, :, rows, :], ub.at[k, dst, :, rows, :],
+                    fr_send.at[k, c, i, j], fr_recv.at[k, c, i, j], move)))
         return out
 
-    def row_copies(k):
-        out = []
-        low, high = pl.ds(8, 8), pl.ds(128, 8)
-        ghost_low, ghost_high = pl.ds(0, 8), pl.ds(136, 8)
-        for i, (step, src, dst) in enumerate(((ROW_DOWN, low, ghost_high), (ROW_UP, high, ghost_low))):
-            out.append((step, remote(
-                ub.at[k, 1:5, :, src, :], ub.at[k, 1:5, :, dst, :], row_send.at[k, i], row_recv.at[k, i], step)))
-        out.append(((1, -1, 0), remote(
-            ub.at[k, 4, :, low, :], ub.at[k, 0, :, ghost_high, :], tr_send.at[k, 0], tr_recv.at[k, 0], (1, -1, 0))))
-        out.append(((-1, 1, 0), remote(
-            ub.at[k, 1, :, high, :], ub.at[k, 5, :, ghost_low, :], tr_send.at[k, 1], tr_recv.at[k, 1], (-1, 1, 0))))
-        return out
+    low, high, ghost_low, ghost_high = pl.ds(8, 8), pl.ds(128, 8), pl.ds(0, 8), pl.ds(136, 8)
+
+    def low_copies(k):
+        c = LOW_CHUNK[k]
+        return [
+            (ROW_DOWN, remote(
+                ub.at[k, 1:5, :, low, :], ub.at[k, 1:5, :, ghost_high, :], row_send.at[k, 0], row_recv.at[k, 0], ROW_DOWN)),
+            ((1, -1, 0), remote(
+                ub.at[k, 4, :, low, :], ub.at[k, 0, :, ghost_high, :], tr_send.at[k, 0], tr_recv.at[k, 0], (1, -1, 0))),
+            ((0, -1, 1), remote(c255.at[k, c], rcp.at[k], rc_send.at[k, 1], rc_recv.at[k, 1], (0, -1, 1))),
+        ]
+
+    def high_copies(k):
+        c = STEPS - 1
+        return [
+            (ROW_UP, remote(
+                ub.at[k, 1:5, :, high, :], ub.at[k, 1:5, :, ghost_low, :], row_send.at[k, 1], row_recv.at[k, 1], ROW_UP)),
+            ((-1, 1, 0), remote(
+                ub.at[k, 1, :, high, :], ub.at[k, 5, :, ghost_low, :], tr_send.at[k, 1], tr_recv.at[k, 1], (-1, 1, 0))),
+            ((0, 1, -1), remote(c0.at[k, c], rcn.at[k], rc_send.at[k, 0], rc_recv.at[k, 0], (0, 1, -1))),
+        ]
 
     def col_copies(k, c):
         return [
@@ -174,13 +208,6 @@
             ((-1, 0, 1), remote(c255.at[k, c], tcp.at[k, c], tc_send.at[k, c, 1], tc_recv.at[k, c, 1], (-1, 0, 1))),
         ]
 
-    def corner_copies(k):
-        c = len(CHUNKS[k]) - 1
-        return [
-            ((0, 1, -1), remote(c0.at[k, c], rcn.at[k], rc_send.at[k, 0], rc_recv.at[k, 0], (0, 1, -1))),
-            ((0, -1, 1), remote(c255.at[k, c], rcp.at[k], rc_send.at[k, 1], rc_recv.at[k, 1], (0, -1, 1))),
-        ]
-
     def start(copies):
         for step, copy in copies:
             @pl.when(exists(step))
@@ -199,10 +226,15 @@
             def _():
                 copy.wait_recv()
 
+    def col_chunks(k):
+        return range(STEPS) if k else range(STEPS - 1, STEPS)
+
     def all_copies(k):
-        out = row_copies(k) + corner_copies(k)
-        for c in range(len(CHUNKS[k])):
-            out += frame_copies(k, c) + col_copies(k, c)
+        out = low_copies(k) + high_copies(k)
+        for c in range(STEPS):
+            out += frame_copies(k, c)
+        for c in col_chunks(k):
+            out += col_copies(k, c)
         return out
 
     def packed_at(t, g):
@@ -238,6 +270,8 @@
         x = [[ub[k, t, h, rows, :] for h in range(2)] for t in range(frames[0], 6)]
         for t in frames:
             here, later = x[t - frames[0]], x[t - frames[0] + 1]
+            if t == 4:
+                later = [jnp.where(last_tm, here[h], later[h]) for h in range(2)]
             rolled = [pltpu.roll(here[h], 127, 1) for h in range(2)]
             after = [
                 jnp.where(last_lane, rolled[1], rolled[0]),
@@ -247,6 +281,8 @@
                 g = [later[h] - here[h], ub[k, t, h, below, :] - here[h], after[h] - here[h]]
                 m = None if k == 0 else [p[d, t, h, rows, :] + SIGMA * g[d] for d in range(3)]
                 new, length = project(k, m, g)
+                if t == 0:
+                    new[0] = jnp.where(first_tm, 0.0, new[0])
                 for d in range(3):
                     p[d, t, h, rows, :] = new[d]
                 if total is None or t == 0:
@@ -267,10 +303,10 @@
                     total = total + square * lax.rsqrt(jnp.maximum(square, TINY))
         return total
 
-    def dual_range(k, c, g0, g1, total):
+    def dual_range(k, b, g0, g1, total):
         def body(g, total):
             rows = rows_of(g)
-            nexts, frame_nexts = cn[k, c], tcn[k, c]
+            nexts, frame_nexts = cn[k, b], tcn[k, b]
 
             def ghost_of(t):
                 if t == 0:
@@ -290,16 +326,18 @@
                 lambda t: pltpu.roll(nexts, 127 - packed_at(t, 15), 1), None,
             )
 
-    def dual_left(k, c):
-        here, below_left, later_left = cp[k, c], rcp[k], tcp[k, c]
+    def dual_left(k, b, last):
+        here, later_left = cp[k, b], tcp[k, b]
         later = jnp.where(lane >= 48, pltpu.roll(later_left, 48, 1), pltpu.roll(here, 112, 1))
         later = jnp.where(jnp.logical_and(lane >= 48, last_tm), here, later)
         last_group = jnp.bitwise_and(lane, 15) == 15
-        follow = jnp.where(last_group, pltpu.roll(below_left, 15, 1), pltpu.roll(here, 127, 1))
+        follow = pltpu.roll(here, 127, 1)
+        if last:
+            follow = jnp.where(last_group, pltpu.roll(rcp[k], 15, 1), follow)
         below = jnp.where(sublane == 7, pltpu.roll(follow, 7, 0), pltpu.roll(here, 7, 0))
         bottom = jnp.logical_and(jnp.logical_and(sublane == 7, last_group), last_row)
         below = jnp.where(bottom, here, below)
-        g = [later - here, below - here, c0[k, c] - here]
+        g = [later - here, below - here, c0[k, b] - here]
         m = None if k == 0 else [pc[k, d] + SIGMA * g[d] for d in range(3)]
         new, _ = project(k, m, g)
         for d in range(3):
@@ -344,8 +382,8 @@
         return grouped(g0, g1, body, total, UNROLL)
 
     def weights():
-        for h in range(2):
-            loads[2 * h + 1].wait()
+        for load in fid_loads:
+            load.wait()
 
         @pl.loop(0, GROUPS)
         def _(g):
@@ -357,67 +395,61 @@
                     inv_fid[t, h, own, :] = 0.5 / lam
                     fid[t, h, own, :] = 0.5 * lam
 
-    def send(k, c, held):
-        c0[k, c], c255[k, c] = held
-        start(frame_copies(k, c) + col_copies(k, c))
-        if c == len(CHUNKS[k]) - 1:
-            start(row_copies(k) + corner_copies(k))
-
-    for h in range(2):
-        loads[2 * h].wait()
-    held = pack(0, 0, GROUPS, (zero, zero))
+    for t in (0, 3):
+        for h in range(2):
+            frame_loads[t, h].wait()
     pl.semaphore_wait(barrier, arrivals)
+    for c in range(STEPS):
+        start(frame_copies(0, c))
     tell(0)
-    for c in range(len(CHUNKS[0])):
-        send(0, c, held)
+    for t in (1, 2):
+        for h in range(2):
+            frame_loads[t, h].wait()
+    c0[0, STEPS - 1], c255[0, STEPS - 1] = pack(0, 0, GROUPS, (zero, zero))
+    start(low_copies(0) + high_copies(0) + col_copies(0, STEPS - 1))
     weights()
-
     hear(0)
     tell(1)
 
     sums = []
     for k in range(ITERS):
         length, total, held = zero, zero, (zero, zero)
-        for c in range(len(CHUNKS[k])):
-            if c == 0:
-                wait_received(row_copies(k) + corner_copies(k))
-            wait_received(frame_copies(k, c) + col_copies(k, c))
-
-            @pl.when(last_tm)
-            def _():
-                ub[k, 5] = ub[k, 4]
-
-            @pl.when(last_row)
-            def _():
-                for t in range(5):
-                    for h in range(2):
-                        ub[k, t, h, 136:137, :] = ub[k, t, h, 135:136, :]
-
-            if c == 0:
+        for c in range(STEPS):
+            final = c == STEPS - 1
+            b = c if k else STEPS - 1
+            wait_received(frame_copies(k, c))
+            if k or c == 0:
+                wait_received(col_copies(k, b))
+            if c == ABOVE_STEP[k]:
+                wait_received(high_copies(k))
+                dual_above(k)
+            if final:
+                wait_received(low_copies(k))
                 hear(k + 1)
                 tell(k + 2)
-            dual_left(k, c)
-            if c == 0:
-                dual_above(k)
-            length = dual_range(k, c, *DUAL_STEPS[k][c], length)
-
-            @pl.when(first_tm)
-            def _():
-                p[0, 0] = jnp.zeros_like(p[0, 0])
-
+
+                @pl.when(last_row)
+                def _():
+                    for t in range(5):
+                        for h in range(2):
+                            ub[k, t, h, 136:137, :] = ub[k, t, h, 135:136, :]
+
+            dual_left(k, b, final)
+            for span in DUAL_STEPS[k][c]:
+                length = dual_range(k, b, *span, length)
             for span in PRIMAL_STEPS[k][c]:
                 total = primal_range(k, *span, total)
-                if k < ITERS - 1:
-                    held = pack(k + 1, *span, held)
-            if k < ITERS - 1:
-                send(k + 1, c, held)
+            if k == ITERS - 1:
+                continue
+            for span in CHUNKS[k + 1][c]:
+                held = pack(k + 1, *span, held)
+            c0[k + 1, c], c255[k + 1, c] = held
+            start(frame_copies(k + 1, c) + col_copies(k + 1, c))
+            if c == LOW_CHUNK[k + 1]:
+                start(low_copies(k + 1))
+            if final:
+                start(high_copies(k + 1))
         sums.append(total + (1.0 if k == 0 else 0.5) * length)
-
-    puts = [
-        pltpu.make_async_copy(out_v.at[:, h], out_hbm.at[:, :, pl.ds(128 * h, 128)], out_sem.at[h]) for h in range(2)
-    ]
-    for put in puts:
-        put.start()
 
     row = jnp.zeros((1, 128), F32)
     row_lane = lax.broadcasted_iota(jnp.int32, (1, 128), 1)
@@ -435,6 +467,9 @@
                 device_id=ring(**{name: j}), device_id_type=MESH,
             ).start()
 
+        if i == 0:
+            for k in range(ITERS):
+                wait_sent(all_copies(k))
         landed = slots.at[pl.ds(0, count - 1)]
         pltpu.make_async_copy(landed, landed, ar_recv.at[i]).wait()
         got = slots[0]
@@ -452,29 +487,34 @@
     cells = float(4 * 128 * 256) * float(n_tm * n_row * n_col)
     gaps_ref[...] = row * (1.0 / cells)
 
-    for k in range(ITERS):
-        wait_sent(all_copies(k))
     drain(by_col, n_col, 0)
     drain(by_tm, n_tm, 1)
     drain(by_row, n_row, 2)
+
+
+def put_out(out_v, gaps_ref, out_hbm, gaps_out, sem):
+    puts = [pltpu.make_async_copy(out_v.at[:, h], out_hbm.at[:, :, pl.ds(128 * h, 128)], sem.at[h]) for h in range(2)]
+    for put in puts:
+        put.start()
+    for k in range(ITERS):
+        gaps_out[k] = gaps_ref[0, k]
     for put in puts:
         put.wait()
 
 
 def on_device(sizes, noisy_video, fidelity):
-    n_chunks = max(len(c) for c in CHUNKS)
+    n_chunks = STEPS
     dma = pltpu.SemaphoreType.DMA
     vmem = lambda *shape: pltpu.VMEM(shape, F32)
     out, gaps = pl.pallas_call(
         functools.partial(kernel, sizes),
-        out_shape=(jax.ShapeDtypeStruct(noisy_video.shape, F32), jax.ShapeDtypeStruct((1, 128), F32)),
+        out_shape=(vmem(4, 2, 128, 128), vmem(1, 128)),
         in_specs=[pl.BlockSpec(memory_space=pl.ANY)] * 2,
-        out_specs=(pl.BlockSpec(memory_space=pl.ANY), pl.BlockSpec(memory_space=pltpu.VMEM)),
+        out_specs=(pl.BlockSpec(memory_space=pltpu.VMEM), pl.BlockSpec(memory_space=pltpu.VMEM)),
         scratch_shapes=[
             vmem(3, 6, 2, 144, 128),
             vmem(3, 5, 2, 136, 128),
             vmem(3, 4, 2, 128, 128),
-            vmem(4, 2, 128, 128),
             vmem(4, 2, 128, 128),
             vmem(4, 2, 128, 128),
             vmem(4, 2, 128, 128),
@@ -492,9 +532,8 @@
             vmem(sizes[2], 1, 128),
             vmem(sizes[0], 1, 128),
             vmem(sizes[1], 1, 128),
-            dma((4,)),
-            dma((2,)),
-            dma((3, n_chunks, 2)), dma((3, n_chunks, 2)),
+            dma((5, 2)),
+            dma((3, n_chunks, 2, 2)), dma((3, n_chunks, 2, 2)),
             dma((3, 2)), dma((3, 2)),
             dma((3, n_chunks, 2)), dma((3, n_chunks, 2)),
             dma((3, 2)), dma((3, 2)),
@@ -505,7 +544,13 @@
         ],
         compiler_params=pltpu.CompilerParams(collective_id=0, has_side_effects=True),
     )(noisy_video, fidelity)
-    return out, gaps[0, :3]
+    return pl.pallas_call(
+        put_out,
+        out_shape=(jax.ShapeDtypeStruct(noisy_video.shape, F32), jax.ShapeDtypeStruct((ITERS,), F32)),
+        in_specs=[pl.BlockSpec(memory_space=pltpu.VMEM)] * 2,
+        out_specs=(pl.BlockSpec(memory_space=pl.ANY), pl.BlockSpec(memory_space=pltpu.SMEM)),
+        scratch_shapes=[dma((2,))],
+    )(*(pltpu.with_memory_space_constraint(x, pltpu.VMEM) for x in (out, gaps)))
 
 
 def solution(mesh):

time: 52.1 us -> 46.5 us (0.89)
  local copies, waits for them, and re-layouts: 3.04 us -> 0 us
  Pallas kernels: 48 us -> 45.8 us
    unnamed x3 -> x0, local copies, waits for them, and re-layouts: 2.53 us -> none
    pallas_call x1 -> x2, Pallas kernels: 48 us -> 45.8 us  [the longest x1 44.4 us: on_device(): pl.pallas_call(functools.partial(kernel, sizes), out_shape=(vmem(4, 2, 12...]
where the time goes in v3:
time: 46.5 us; the launch traced here: 46.4 us
  Pallas kernels  45.8 us (98%)
  between operations  0.64 us (1%)
    pallas_call x1, Pallas kernels, on_device(): pl.pallas_call(functools.partial(kernel, sizes), out_shape=(vmem(4, 2, 12...  44.4 us
    pallas_call x1, Pallas kernels, on_device(): pl.pallas_call(put_out, out_shape=(jax.ShapeDtypeStruct(noisy_video.shape...  1.33 us

profile of v3, /device:TPU:1, one launch (start us, length us, event | category | flops | bytes accessed | tf_op | source)
XLA Modules:
  0.0 46.4 jit_solution(16002010982040116106)
XLA Ops:
  0.6 44.4 %shard_map.41 = (f32[4,2,128,128]{3,2,1,0:T(8,128)S(1)}, f32[1,128]{1,0:T(1,128)S(1)}) custom-call(f32[4,128,256]{2,1,0:T(8,128)} %f_hbm.1, f32[4,128,256]{2,1,0:T(8,128)} %fid_hbm.1), custom_call_target="tpu_custom_call" | custom-call | tf_op jit(solution)/shard_map/pallas_call | solution.py:509
  45.1 1.3 %shard_map.42 = (f32[4,128,256]{2,1,0:T(8,128)}, f32[3]{0:T(128)}) custom-call(f32[4,2,128,128]{3,2,1,0:T(8,128)S(1)} %get-tuple-element.4.out_v, f32[1,128]{1,0:T(1,128)S(1)} %get-tuple-element.5.gaps_ref), custom_call_target="tpu_custom_call" | custom-call | tf_op jit(solution)/shard_map/pallas_call | solution.py:547

commit v4 on v3

--- a/solution.py
+++ b/solution.py
@@ -25,27 +25,26 @@
     (1, -1, 0), (-1, 1, 0), (1, 0, -1), (-1, 0, 1), (0, 1, -1), (0, -1, 1),
 )
 
-CHUNKS = (
-    ([(0, 5)], [(5, 9)], [(9, 13)], [(13, 16)]),
-    ([(0, 4)], [(4, 8)], [(8, 12)], [(12, 16)]),
-    ([(1, 3)], [(3, 7)], [(7, 11)], [(11, 16), (0, 1)]),
-)
-DUAL_STEPS = (
-    ([(0, 4)], [(4, 8)], [(8, 12)], [(12, 16)]),
-    ([(0, 3)], [(3, 7)], [(7, 11)], [(11, 16)]),
-    ([(1, 2)], [(2, 6)], [(6, 10)], [(10, 16), (0, 1)]),
-)
-PRIMAL_STEPS = (
-    ([(0, 4)], [(4, 8)], [(8, 12)], [(12, 16)]),
-    ([(1, 3)], [(3, 7)], [(7, 11)], [(11, 16), (0, 1)]),
-    ([], [(2, 6)], [(6, 10)], [(10, 16), (0, 2)]),
-)
-STEPS = 4
-ABOVE_STEP = (0, 3, 3)
-LOW_CHUNK = (3, 0, 3)
+CUTS = (6, 11)
+STEPS = len(CUTS) + 1
+
+
+def spans(first, back, *more):
+    edges = [first] + [cut - back for cut in CUTS] + [16]
+    out = [[(a, b)] if b > a else [] for a, b in zip(edges, edges[1:])]
+    out[-1] += more
+    return out
+
+
+CHUNKS = (spans(0, -1), spans(0, 0), spans(1, 1, (0, 1)))
+DUAL_STEPS = (spans(0, 0), spans(0, 1), spans(1, 2, (0, 1)))
+PRIMAL_STEPS = (spans(0, 0), spans(1, 1, (0, 1)), spans(2, 2, (0, 2)))
+PHASES = (("x", "tm", "core"), ("row",))
+ABOVE_STEP = (0, STEPS - 1, STEPS - 1)
+LOW_CHUNK = (STEPS - 1, 0, STEPS - 1)
 
 UNROLL = 4
-PACK_UNROLL = 5
+PACK_UNROLL = 16
 
 
 def grouped(g0, g1, body, carry, unroll):
@@ -72,12 +71,13 @@
 
 def kernel(
     sizes, f_hbm, fid_hbm, out_v, gaps_ref,
-    ub, p, gu, res, damp, inv_fid, fid, c0, c255, cn, cp, tcn, tcp, rcn, rcp, pc, part, by_col, by_tm, by_row,
+    ub, p, gu, res, damp, inv_fid, fid, c0, c255, cn, cp, tcn, tcp, rcn, rcp, pc, part, by_phase0, by_phase1, by_phase2,
     load_sem,
     fr_send, fr_recv, row_send, row_recv, col_send, col_recv, tr_send, tr_recv, tc_send, tc_recv, rc_send, rc_recv,
     ar_send, ar_recv, token_sem,
 ):
     n_tm, n_row, n_col = sizes
+    by_phase = (by_phase0, by_phase1, by_phase2)
     at = (lax.axis_index("tm"), lax.axis_index("row"), lax.axis_index("col"))
 
     def there(step):
@@ -140,7 +140,8 @@
             reach *= 2
         return out
 
-    rounds = list(zip_longest(tokens("row", n_row), tokens("col", n_col), tokens("tm", n_tm)))
+    of_rows, of_cols = tokens("row", n_row), tokens("col", n_col)
+    rounds = list(zip_longest(of_rows, of_cols + [("tm", 1)] * (n_tm // 2)))
 
     def tell(i):
         for j, token in enumerate(rounds[i] if i < len(rounds) else ()):
@@ -178,7 +179,7 @@
                     fr_send.at[k, c, i, j], fr_recv.at[k, c, i, j], move)))
         return out
 
-    low, high, ghost_low, ghost_high = pl.ds(8, 8), pl.ds(128, 8), pl.ds(0, 8), pl.ds(136, 8)
+    low, high, ghost_low, ghost_high = pl.ds(8, 1), pl.ds(135, 1), pl.ds(7, 1), pl.ds(136, 1)
 
     def low_copies(k):
         c = LOW_CHUNK[k]
@@ -395,23 +396,22 @@
                     inv_fid[t, h, own, :] = 0.5 / lam
                     fid[t, h, own, :] = 0.5 * lam
 
-    for t in (0, 3):
-        for h in range(2):
-            frame_loads[t, h].wait()
+    for load in frame_loads.values():
+        load.wait()
+    c0[0, STEPS - 1], c255[0, STEPS - 1] = pack(0, 0, GROUPS, (zero, zero))
     pl.semaphore_wait(barrier, arrivals)
-    for c in range(STEPS):
+    start(col_copies(0, STEPS - 1))
+    start(frame_copies(0, 0))
+    start(low_copies(0) + high_copies(0))
+    tell(0)
+    for c in range(1, STEPS):
         start(frame_copies(0, c))
-    tell(0)
-    for t in (1, 2):
-        for h in range(2):
-            frame_loads[t, h].wait()
-    c0[0, STEPS - 1], c255[0, STEPS - 1] = pack(0, 0, GROUPS, (zero, zero))
-    start(low_copies(0) + high_copies(0) + col_copies(0, STEPS - 1))
     weights()
     hear(0)
     tell(1)
 
-    sums = []
+    row = jnp.zeros((1, 128), F32)
+    row_lane = lax.broadcasted_iota(jnp.int32, (1, 128), 1)
     for k in range(ITERS):
         length, total, held = zero, zero, (zero, zero)
         for c in range(STEPS):
@@ -444,52 +444,66 @@
             for span in CHUNKS[k + 1][c]:
                 held = pack(k + 1, *span, held)
             c0[k + 1, c], c255[k + 1, c] = held
-            start(frame_copies(k + 1, c) + col_copies(k + 1, c))
+            start(col_copies(k + 1, c))
             if c == LOW_CHUNK[k + 1]:
                 start(low_copies(k + 1))
             if final:
                 start(high_copies(k + 1))
-        sums.append(total + (1.0 if k == 0 else 0.5) * length)
-
-    row = jnp.zeros((1, 128), F32)
-    row_lane = lax.broadcasted_iota(jnp.int32, (1, 128), 1)
-    for k in range(ITERS):
-        row = jnp.where(row_lane == k, jnp.sum(sums[k]), row)
-
-    def exchange(mine, slots, me, count, name, i, row):
-        mine[...] = row
+            start(frame_copies(k + 1, c))
+        row = jnp.where(row_lane == k, jnp.sum(total + (1.0 if k == 0 else 0.5) * length), row)
+
+    places = {"tm": (at[0], n_tm), "row": (at[1], n_row), "x": (at[2] // 2, n_col // 2), "core": (at[2] % 2, 2)}
+
+    def exchange(i, axes, row):
+        slots, count, me = by_phase[i], 1, 0
+        for name in axes:
+            pos, size = places[name]
+            count, me = count * size, me * size + pos
+        part[i] = row
         slots[me] = row
 
-        @pl.loop(1, count)
-        def _(j):
+        def tell_one(j):
+            there, left = {name: places[name][0] for name in places}, j
+            for name in reversed(axes):
+                size = places[name][1]
+                there[name] = jnp.bitwise_xor(there[name], jnp.bitwise_and(left, size - 1))
+                left = jnp.right_shift(left, size.bit_length() - 1)
             pltpu.make_async_remote_copy(
-                src_ref=mine, dst_ref=slots.at[me], send_sem=ar_send.at[i], recv_sem=ar_recv.at[i],
-                device_id=ring(**{name: j}), device_id_type=MESH,
+                src_ref=part.at[i], dst_ref=slots.at[me], send_sem=ar_send.at[i], recv_sem=ar_recv.at[i],
+                device_id=dict(tm=there["tm"], row=there["row"], col=there["x"] * 2 + there["core"]),
+                device_id_type=MESH,
             ).start()
+
+        if count <= 16:
+            for j in range(1, count):
+                tell_one(j)
+        else:
+            pl.loop(1, count)(tell_one)
 
         if i == 0:
             for k in range(ITERS):
                 wait_sent(all_copies(k))
         landed = slots.at[pl.ds(0, count - 1)]
         pltpu.make_async_copy(landed, landed, ar_recv.at[i]).wait()
-        got = slots[0]
-        for j in range(1, count):
-            got = got + slots[j]
-        return got
-
-    def drain(slots, count, i):
-        landed = slots.at[pl.ds(0, count - 1)]
+        got = [slots[j] for j in range(count)]
+        while len(got) > 1:
+            got = [got[j] + got[j + 1] for j in range(0, len(got), 2)]
+        return got[0]
+
+    def drain(i, axes):
+        count = 1
+        for name in axes:
+            count *= places[name][1]
+        landed = by_phase[i].at[pl.ds(0, count - 1)]
         pltpu.make_async_copy(landed, landed, ar_send.at[i]).wait()
 
-    row = exchange(part.at[0], by_col, at[2], n_col, "col", 0, row)
-    row = exchange(part.at[1], by_tm, at[0], n_tm, "tm", 1, row)
-    row = exchange(part.at[2], by_row, at[1], n_row, "row", 2, row)
+    for i, axes in enumerate(PHASES):
+        row = exchange(i, axes, row)
     cells = float(4 * 128 * 256) * float(n_tm * n_row * n_col)
     gaps_ref[...] = row * (1.0 / cells)
 
-    drain(by_col, n_col, 0)
-    drain(by_tm, n_tm, 1)
-    drain(by_row, n_row, 2)
+    for i, axes in enumerate(PHASES):
+        drain(i, axes)
 
 
 def put_out(out_v, gaps_ref, out_hbm, gaps_out, sem):
@@ -529,9 +543,9 @@
             vmem(3, 8, 128),
             vmem(4, 4, 8, 128),
             vmem(3, 1, 128),
-            vmem(sizes[2], 1, 128),
-            vmem(sizes[0], 1, 128),
-            vmem(sizes[1], 1, 128),
+            vmem(64, 1, 128),
+            vmem(64, 1, 128),
+            vmem(64, 1, 128),
             dma((5, 2)),
             dma((3, n_chunks, 2, 2)), dma((3, n_chunks, 2, 2)),
             dma((3, 2)), dma((3, 2)),

time: 46.5 us -> 43.4 us (0.933)
  Pallas kernels: 45.8 us -> 42.7 us
    pallas_call x1, Pallas kernels: 44.4 us -> 41.3 us  [on_device(): pl.pallas_call(functools.partial(kernel, sizes), out_shape=(vmem(4, 2, 12...]
where the time goes in v4:
time: 43.4 us; the launch traced here: 43.3 us
  Pallas kernels  42.7 us (98%)
  between operations  0.64 us (1%)
    pallas_call x1, Pallas kernels, on_device(): pl.pallas_call(functools.partial(kernel, sizes), out_shape=(vmem(4, 2, 12...  41.3 us
    pallas_call x1, Pallas kernels, on_device(): pl.pallas_call(put_out, out_shape=(jax.ShapeDtypeStruct(noisy_video.shape...  1.33 us

profile of v4, /device:TPU:1, one launch (start us, length us, event | category | flops | bytes accessed | tf_op | source)
XLA Modules:
  0.0 43.3 jit_solution(14382445746011517707)
XLA Ops:
  0.6 41.3 %shard_map.41 = (f32[4,2,128,128]{3,2,1,0:T(8,128)S(1)}, f32[1,128]{1,0:T(1,128)S(1)}) custom-call(f32[4,128,256]{2,1,0:T(8,128)} %f_hbm.1, f32[4,128,256]{2,1,0:T(8,128)} %fid_hbm.1), custom_call_target="tpu_custom_call" | custom-call | tf_op jit(solution)/shard_map/pallas_call | solution.py:523
  42.0 1.3 %shard_map.42 = (f32[4,128,256]{2,1,0:T(8,128)}, f32[3]{0:T(128)}) custom-call(f32[4,2,128,128]{3,2,1,0:T(8,128)S(1)} %get-tuple-element.4.out_v, f32[1,128]{1,0:T(1,128)S(1)} %get-tuple-element.5.gaps_ref), custom_call_target="tpu_custom_call" | custom-call | tf_op jit(solution)/shard_map/pallas_call | solution.py:561

commit v5 on v4

--- a/solution.py
+++ b/solution.py
@@ -25,7 +25,7 @@
     (1, -1, 0), (-1, 1, 0), (1, 0, -1), (-1, 0, 1), (0, 1, -1), (0, -1, 1),
 )
 
-CUTS = (6, 11)
+CUTS = (5, 11)
 STEPS = len(CUTS) + 1
 
 
@@ -506,12 +506,15 @@
         drain(i, axes)
 
 
-def put_out(out_v, gaps_ref, out_hbm, gaps_out, sem):
+def put_out(out_v, gaps_ref, out_hbm, gaps_out, sem, gaps_s):
     puts = [pltpu.make_async_copy(out_v.at[:, h], out_hbm.at[:, :, pl.ds(128 * h, 128)], sem.at[h]) for h in range(2)]
     for put in puts:
         put.start()
     for k in range(ITERS):
-        gaps_out[k] = gaps_ref[0, k]
+        gaps_s[k] = gaps_ref[0, k]
+    last = pltpu.make_async_copy(gaps_s, gaps_out, sem.at[2])
+    last.start()
+    puts.append(last)
     for put in puts:
         put.wait()
 
@@ -562,8 +565,8 @@
         put_out,
         out_shape=(jax.ShapeDtypeStruct(noisy_video.shape, F32), jax.ShapeDtypeStruct((ITERS,), F32)),
         in_specs=[pl.BlockSpec(memory_space=pltpu.VMEM)] * 2,
-        out_specs=(pl.BlockSpec(memory_space=pl.ANY), pl.BlockSpec(memory_space=pltpu.SMEM)),
-        scratch_shapes=[dma((2,))],
+        out_specs=(pl.BlockSpec(memory_space=pl.ANY), pl.BlockSpec(memory_space=pl.ANY)),
+        scratch_shapes=[dma((3,)), pltpu.SMEM((ITERS,), F32)],
     )(*(pltpu.with_memory_space_constraint(x, pltpu.VMEM) for x in (out, gaps)))
 
 

time: 43.4 us -> 43.1 us (level)
    pallas_call x1, Pallas kernels: 1.33 us -> 0.83 us  [on_device(): pl.pallas_call(put_out, out_shape=(jax.ShapeDtypeStruct(noisy_video.shape...]
where the time goes in v5:
time: 43.1 us; the launch traced here: 42.9 us
  Pallas kernels  42.3 us (98%)
  between operations  0.64 us (1%)
    pallas_call x1, Pallas kernels, on_device(): pl.pallas_call(functools.partial(kernel, sizes), out_shape=(vmem(4, 2, 12...  41.5 us

profile of v5, /device:TPU:1, one launch (start us, length us, event | category | flops | bytes accessed | tf_op | source)
XLA Modules:
  0.0 42.9 jit_solution(7743230155712545491)
XLA Ops:
  0.6 41.5 %shard_map.41 = (f32[4,2,128,128]{3,2,1,0:T(8,128)S(1)}, f32[1,128]{1,0:T(1,128)S(1)}) custom-call(f32[4,128,256]{2,1,0:T(8,128)} %f_hbm.1, f32[4,128,256]{2,1,0:T(8,128)} %fid_hbm.1), custom_call_target="tpu_custom_call" | custom-call | tf_op jit(solution)/shard_map/pallas_call | solution.py:526
  42.1 0.8 %shard_map.42 = (f32[4,128,256]{2,1,0:T(8,128)}, f32[3]{0:T(128)}) custom-call(f32[4,2,128,128]{3,2,1,0:T(8,128)S(1)} %get-tuple-element.4.out_v, f32[1,128]{1,0:T(1,128)S(1)} %get-tuple-element.5.gaps_ref), custom_call_target="tpu_custom_call" | custom-call | tf_op jit(solution)/shard_map/pallas_call | solution.py:564

commit v6 on v5

--- a/solution.py
+++ b/solution.py
@@ -450,7 +450,8 @@
             if final:
                 start(high_copies(k + 1))
             start(frame_copies(k + 1, c))
-        row = jnp.where(row_lane == k, jnp.sum(total + (1.0 if k == 0 else 0.5) * length), row)
+        share = jnp.sum(total + (1.0 if k == 0 else 0.5) * length, axis=0, keepdims=True)
+        row = jnp.where(row_lane == k, jnp.sum(share, axis=1, keepdims=True), row)
 
     places = {"tm": (at[0], n_tm), "row": (at[1], n_row), "x": (at[2] // 2, n_col // 2), "core": (at[2] % 2, 2)}
 
@@ -466,7 +467,8 @@
             there, left = {name: places[name][0] for name in places}, j
             for name in reversed(axes):
                 size = places[name][1]
-                there[name] = jnp.bitwise_xor(there[name], jnp.bitwise_and(left, size - 1))
+                off = jnp.bitwise_and(left, size - 1)
+                there[name] = jnp.bitwise_and(there[name] + off, size - 1) if axes == ("row",) else jnp.bitwise_xor(there[name], off)
                 left = jnp.right_shift(left, size.bit_length() - 1)
             pltpu.make_async_remote_copy(
                 src_ref=part.at[i], dst_ref=slots.at[me], send_sem=ar_send.at[i], recv_sem=ar_recv.at[i],
@@ -474,11 +476,11 @@
                 device_id_type=MESH,
             ).start()
 
-        if count <= 16:
-            for j in range(1, count):
+        if axes == ("row",):
+            for j in sorted(range(1, count), key=lambda j: -min(j, count - j)):
                 tell_one(j)
         else:
-            pl.loop(1, count)(tell_one)
+            pl.loop(1, count)(lambda j: tell_one(count - j))
 
         if i == 0:
             for k in range(ITERS):

time: 43.1 us -> 42.8 us (level)
  no operation moved by 1% of the time
where the time goes in v6:
time: 42.8 us; the launch traced here: 42.6 us
  Pallas kernels  42 us (98%)
  between operations  0.64 us (1%)
    pallas_call x1, Pallas kernels, on_device(): pl.pallas_call(functools.partial(kernel, sizes), out_shape=(vmem(4, 2, 12...  41.2 us

profile of v6, /device:TPU:1, one launch (start us, length us, event | category | flops | bytes accessed | tf_op | source)
XLA Modules:
  0.0 42.6 jit_solution(2561161029233428204)
XLA Ops:
  0.6 41.2 %shard_map.41 = (f32[4,2,128,128]{3,2,1,0:T(8,128)S(1)}, f32[1,128]{1,0:T(1,128)S(1)}) custom-call(f32[4,128,256]{2,1,0:T(8,128)} %f_hbm.1, f32[4,128,256]{2,1,0:T(8,128)} %fid_hbm.1), custom_call_target="tpu_custom_call" | custom-call | tf_op jit(solution)/shard_map/pallas_call | solution.py:528
  41.8 0.8 %shard_map.42 = (f32[4,128,256]{2,1,0:T(8,128)}, f32[3]{0:T(128)}) custom-call(f32[4,2,128,128]{3,2,1,0:T(8,128)S(1)} %get-tuple-element.4.out_v, f32[1,128]{1,0:T(1,128)S(1)} %get-tuple-element.5.gaps_ref), custom_call_target="tpu_custom_call" | custom-call | tf_op jit(solution)/shard_map/pallas_call | solution.py:566

commit v7 on v6

--- a/solution.py
+++ b/solution.py
@@ -43,7 +43,7 @@
 ABOVE_STEP = (0, STEPS - 1, STEPS - 1)
 LOW_CHUNK = (STEPS - 1, 0, STEPS - 1)
 
-UNROLL = 4
+UNROLL = 6
 PACK_UNROLL = 16
 
 

time: 42.8 us -> 42.8 us (level)
  no operation moved by 1% of the time
where the time goes in v7:
time: 42.8 us; the launch traced here: 42.6 us
  Pallas kernels  42 us (98%)
  between operations  0.64 us (1%)
    pallas_call x1, Pallas kernels, on_device(): pl.pallas_call(functools.partial(kernel, sizes), out_shape=(vmem(4, 2, 12...  41.2 us

profile of v7, /device:TPU:1, one launch (start us, length us, event | category | flops | bytes accessed | tf_op | source)
XLA Modules:
  0.0 42.6 jit_solution(2561161029233428204)
XLA Ops:
  0.6 41.2 %shard_map.41 = (f32[4,2,128,128]{3,2,1,0:T(8,128)S(1)}, f32[1,128]{1,0:T(1,128)S(1)}) custom-call(f32[4,128,256]{2,1,0:T(8,128)} %f_hbm.1, f32[4,128,256]{2,1,0:T(8,128)} %fid_hbm.1), custom_call_target="tpu_custom_call" | custom-call | tf_op jit(solution)/shard_map/pallas_call | solution.py:528
  41.8 0.8 %shard_map.42 = (f32[4,128,256]{2,1,0:T(8,128)}, f32[3]{0:T(128)}) custom-call(f32[4,2,128,128]{3,2,1,0:T(8,128)S(1)} %get-tuple-element.4.out_v, f32[1,128]{1,0:T(1,128)S(1)} %get-tuple-element.5.gaps_ref), custom_call_target="tpu_custom_call" | custom-call | tf_op jit(solution)/shard_map/pallas_call | solution.py:566
